TPU v7x, 32 devices: a whole 2x2x4 slice. The times are simulated.
32 devices in a mesh: dp: 2 (over x), tp: 16 (over y, z, core).
Axes of the slice: x: 2, y: 2, z: 4, core: 2. Of those that a mesh axis runs over, the one named last changes fastest.
Arguments:
- x: bfloat16 [13312, 2560], P(('dp', 'tp')), parts along dimension 0
- dy: bfloat16 [13312, 2560], P(('dp', 'tp')), parts along dimension 0
- gate: bfloat16 [13312, 10240], P('dp', 'tp'), parts along dimension 0
- up: bfloat16 [13312, 10240], P('dp', 'tp'), parts along dimension 0
- w_gate: bfloat16 [2560, 10240], P(None, 'tp')
- w_up: bfloat16 [2560, 10240], P(None, 'tp')
- w_down: bfloat16 [10240, 2560], P('tp')
Outputs:
- output 1: bfloat16 [13312, 2560], P(('dp', 'tp')), parts along dimension 0
- output 2: bfloat16 [5120, 10240], P('dp', 'tp'), parts along dimension 0
- output 3: bfloat16 [5120, 10240], P('dp', 'tp'), parts along dimension 0
- output 4: bfloat16 [20480, 2560], P(('dp', 'tp')), parts along dimension 0
There are 2 independent parts. A program takes and returns all parts, laid end to end along the dimension named above; an argument that names none is the same for every part.
All inputs are finite; a program needn't handle non-finite values.
Results may differ from a plain program's by a relative error of at most 0.012.
Values are sent between devices in bfloat16 or wider.
A program may use at most 2 GiB of HBM per device.

v0:
```python
import jax
import jax.numpy as jnp


def act(gate, up):
    return jax.nn.gelu(gate) * up


def solution(mesh):
    def step(x, dy, gate, up, w_gate, w_up, w_down):
        hidden, back = jax.vjp(act, gate.astype(jnp.float32), up.astype(jnp.float32))
        d_hidden = jnp.dot(dy, w_down.T, preferred_element_type=jnp.float32)
        d_gate, d_up = (g.astype(jnp.bfloat16) for g in back(d_hidden))
        dx = jnp.dot(d_gate, w_gate.T) + jnp.dot(d_up, w_up.T)
        groups = mesh.shape["dp"]

        def by_group(a, b):
            a, b = (t.reshape(groups, -1, t.shape[-1]) for t in (a, b))
            product = jnp.einsum("gta,gtb->gab", a, b, preferred_element_type=jnp.float32)
            return product.astype(jnp.bfloat16).reshape(-1, b.shape[-1])

        return dx, by_group(x, d_gate), by_group(x, d_up), by_group(hidden.astype(jnp.bfloat16), dy)

    return step
```

profile of v0, /device:TPU:0, one launch (start us, length us, event | category | flops | bytes accessed | tf_op | source)
XLA Modules:
  0.0 699.9 jit_solution(8025572293070950040)
XLA Ops:
  7.2 0.0 copy-start
  7.2 0.0 all-gather.11.cloned.1.call-start
  7.2 0.7 all-gather.11.cloned.1.call-update
  7.9 0.0 all-gather.13.cloned.1.call-start
  8.0 0.7 all-gather.13.cloned.1.call-update
  8.7 0.0 reduce-scatter.4.cloned.1.call-start
  8.7 174.1 %all-gather.11.cloned.1.call-done = bf16[6656,2560]{1,0:T(8,128)(2,1)} async-done(((bf16[416,2560]{1,0:T(8,128)(2,1)}), bf16[6656,2560]{1,0:T(8,128)(2,1)}) %all-gather.11.cloned.1.call-update) | async-done | bytes 34078736 | tf_op args[1]
  182.8 46.1 %fusion.4 = (bf16[6656,640]{1,0:T(8,128)(2,1)}, f32[6656,640]{1,0:T(8,128)}) fusion(bf16[6656,640]{1,0:T(8,128)(2,1)} %param.3, bf16[6656,640]{1,0:T(8,128)(2,1)} %param.2, bf16[6656,2560]{1,0:T(8,128)(2,1)} %all-gather.11.cloned.1.call-done, bf16[640,2560]{1,0:T(8,128)(2,1)} %param.1), kind=kOutput, calls=%fused_computation.12 | convolution fusion | flops 21908357120 | bytes 79953920 | tf_op jit(solution)/dot_general | solution.py:12
  228.9 0.0 copy-done
  228.9 34.2 %fusion.25 = bf16[6656,2560]{1,0:T(8,128)(2,1)} fusion(bf16[6656,640]{1,0:T(8,128)(2,1)} %get-tuple-element.4, bf16[2560,640]{1,0:T(8,128)(2,1)S(1)} %copy-done), kind=kOutput, calls=%fused_computation.33 | convolution fusion | flops 21810380800 | bytes 45875200 | tf_op jit(solution)/dot_general | solution.py:14
  263.1 39.8 %convolution_add_fusion = bf16[6656,2560]{1,0:T(8,128)(2,1)} fusion(bf16[6656,2560]{1,0:T(8,128)(2,1)} %fusion.25, bf16[2560,640]{1,0:T(8,128)(2,1)} %param.5, f32[6656,640]{1,0:T(8,128)} %get-tuple-element.5, bf16[6656,640]{1,0:T(8,128)(2,1)} %param.3), kind=kOutput, calls=%fused_computation | convolution fusion | flops 21874278400 | bytes 96993280 | tf_op jit(solution)/dot_general | solution.py:14
  302.8 0.0 reduce-scatter.4.cloned.1.call-update
  302.8 52.0 %all-gather.13.cloned.1.call-done = bf16[6656,2560]{1,0:T(8,128)(2,1)} async-done(((bf16[416,2560]{1,0:T(8,128)(2,1)}), bf16[6656,2560]{1,0:T(8,128)(2,1)}) %all-gather.13.cloned.1.call-update) | async-done | bytes 34078736 | tf_op jit(solution)/reshape | solution.py:18
  354.8 34.0 %fusion.20 = bf16[2560,640]{0,1:T(8,128)(2,1)S(1)} fusion(bf16[6656,2560]{1,0:T(8,128)(2,1)} %all-gather.13.cloned.1.call-done, f32[6656,640]{1,0:T(8,128)} %get-tuple-element.5, bf16[6656,640]{1,0:T(8,128)(2,1)} %param.3), kind=kOutput, calls=%fused_computation.28 | convolution fusion | flops 21858877440 | bytes 62914560 | tf_op jit(solution)/gta,gtb->gab/dot_general | solution.py:19
  388.8 3.4 copy.1
  392.2 28.4 %fusion.19 = bf16[2560,640]{0,1:T(8,128)(2,1)S(1)} fusion(bf16[6656,640]{1,0:T(8,128)(2,1)} %get-tuple-element.4, bf16[6656,2560]{1,0:T(8,128)(2,1)} %all-gather.13.cloned.1.call-done), kind=kOutput, calls=%fused_computation.27 | convolution fusion | flops 21812019200 | bytes 45875200 | tf_op jit(solution)/gta,gtb->gab/dot_general | solution.py:19
  420.5 3.4 copy
  423.9 0.0 copy-start.1
  423.9 35.9 %fusion.16 = bf16[640,2560]{1,0:T(8,128)(2,1)} fusion(bf16[6656,2560]{1,0:T(8,128)(2,1)} %all-gather.11.cloned.1.call-done, bf16[6656,640]{1,0:T(8,128)(2,1)} %param.2, bf16[6656,640]{1,0:T(8,128)(2,1)} %param.3), kind=kOutput, calls=%fused_computation.26 | convolution fusion | flops 21863137280 | bytes 54394880 | tf_op jit(solution)/gta,gtb->gab/dot_general | solution.py:19
  459.8 233.5 %reduce-scatter.4.cloned.1.call-done = bf16[416,2560]{1,0:T(8,128)(2,1)} async-done(((bf16[6656,2560]{1,0:T(8,128)(2,1)}), bf16[416,2560]{1,0:T(8,128)(2,1)}) %reduce-scatter.4.cloned.1.call-update) | async-done | bytes 2129936
  693.3 0.0 copy-done.1
Async XLA Ops:
  7.2 221.7 %copy-start = (bf16[2560,640]{1,0:T(8,128)(2,1)S(1)}, bf16[2560,640]{1,0:T(8,128)(2,1)}, u32[]{:S(2)}) copy-start(bf16[2560,640]{1,0:T(8,128)(2,1)} %param.4) | copy-start | bytes 9830404
  7.2 175.6 %all-gather.11.cloned.1.call-start = ((), (), s32[]{:S(2)}) async-start(), calls=%async_computation.1 | async-start | bytes 36208640 | tf_op args[1]
  7.9 346.9 %all-gather.13.cloned.1.call-start = ((), (), s32[]{:S(2)}) async-start(), calls=%async_computation.2 | async-start | bytes 36208640 | tf_op jit(solution)/reshape | solution.py:18
  8.7 684.7 %reduce-scatter.4.cloned.1.call-start = ((), (), s32[]{:S(2)}) async-start(), calls=%async_computation.3 | async-start | bytes 36208640
  423.9 269.4 %copy-start.1 = (bf16[2560,640]{1,0:T(8,128)(2,1)S(1)}, bf16[2560,640]{1,0:T(8,128)(2,1)}, u32[]{:S(2)}) copy-start(bf16[2560,640]{1,0:T(8,128)(2,1)} %param.4) | copy-start | bytes 9830404
Sparse Core Ops, SparseCore 0:
  9.6 173.1 all-gather.10
  184.4 170.3 all-gather.12
  359.6 333.6 reduce-scatter.3
where the time goes:
time: 700 us
  waiting for transfers between devices  461 us (66%)
  matrix products  218 us (31%)
  between operations  13.8 us (2%)
    unnamed x5, waiting for transfers between devices  409 us
    dot_general x3, matrix products, by_group(): jnp.einsum('gta,gtb->gab', a, b, preferred_element_type=jnp.float32)  98.2 us
    dot_general x2, matrix products, step(): dx = jnp.dot(d_gate, w_gate.T) + jnp.dot(d_up, w_up.T)  73.9 us
    reshape x1, waiting for transfers between devices, by_group(): a, b = (t.reshape(groups, -1, t.shape[-1]) for t in (a, b))  52 us
    dot_general x1, matrix products, step(): d_hidden = jnp.dot(dy, w_down.T, preferred_element_type=jnp.float32)  46.1 us
  transfers between devices with their start and end apart: 3, of which 3 were waited for; matrix products, arithmetic and copies ran while one was open for 32% of the time, Pallas kernels for 0%

commit v1 on v0

v1 whole, which is shorter than its diff:
```python
import jax
import jax.numpy as jnp
from jax import lax
from jax.experimental import pallas as pl
from jax.experimental.pallas import tpu as pltpu
from jax.sharding import PartitionSpec as P

MESH = pl.DeviceIdType.MESH
F32, BF16 = jnp.float32, jnp.bfloat16

H = 2
SLOTS = 10
P_, D_, Y_, W_ = 0, 1, 2, 3
DY, X = 0, 1
ROLES = ("M", "C")

SENDS = {
    "M": {
        P_: {0: (DY, "00M"), 1: (DY, "01M"), 2: (DY, "01C"), 3: (X, "00M"), 4: (X, "01M"), 5: (X, "01C")},
        D_: {0: (DY, "00M"), 1: (DY, "00C"), 2: (DY, "10M"), 3: (X, "00M"), 4: (X, "00C"), 5: (X, "10M")},
        Y_: {0: (DY, "00M"), 1: (DY, "00C"), 2: (DY, "01C"), 3: (X, "00M"), 4: (X, "00C"), 6: (X, "01C")},
    },
    "C": {
        P_: {0: (DY, "00C"), 1: (X, "00C")},
        Y_: {0: (DY, "00C"), 1: (DY, "00M"), 2: (DY, "01M"), 3: (DY, "01C"),
             4: (X, "00C"), 5: (X, "00M"), 6: (X, "01M"), 7: (X, "01C")},
    },
}
RECEIVES = {
    "M": {
        0: [(DY, "00C"), (DY, "10M"), (DY, "01M")], 1: [(X, "00C"), (DY, "10C"), (DY, "01C")], 2: [(DY, "11C"), (DY, "11M")],
        3: [(X, "10M"), (X, "01M")], 4: [(X, "10C"), (X, "01C")], 5: [(X, "11M")], 6: [(X, "11C")],
    },
    "C": {
        0: [(DY, "00M"), (DY, "10C")], 1: [(DY, "01M"), (DY, "10M")], 2: [(DY, "01C"), (DY, "11M")],
        3: [(DY, "11C"), (X, "00M")], 4: [(X, "10C"), (X, "01M")], 5: [(X, "10M"), (X, "01C")], 6: [(X, "11M")], 7: [(X, "11C")],
    },
}
SUMS = {
    "M": {
        5: [("11M", (P_,), Y_, 0)],
        6: [("11C", (P_,), D_, 0)],
        7: [("01C", (P_,), D_, 1), ("10C", (P_, D_), Y_, 1)],
        8: [("01M", (P_, Y_), D_, 1), ("10M", (P_,), Y_, 1), ("00C", (D_, Y_), P_, 0)],
        9: [("00M", (P_, D_, Y_), None, 0)],
    },
    "C": {
        2: [("10C", (), P_, 0)], 3: [("10M", (), P_, 1)], 4: [("11M", (), P_, 1)], 5: [("11C", (), P_, 1)],
        6: [("01C", (), P_, 1)], 7: [("01M", (), P_, 1)], 8: [("00M", (), P_, 1)], 9: [("00C", (P_,), None, 0)],
    },
}
TOKENS = {
    "M": {
        DY: [["00M"], ["00C", "10M", "01M"], ["10C", "01C"], ["11M", "11C"]],
        X: [["00M", "00C"], ["10M", "01M"], ["01C", "10C"], ["11M", "11C"]],
    },
    "C": {
        DY: [["00C"], ["00M", "10C"], ["01M", "10M"], ["01C", "11M"], ["11C"]],
        X: [["00C", "00M"], ["10C", "01M"], ["01C", "10M"], ["11M", "11C"]],
    },
}
X_FROM = {"M": 9, "C": 11}


def pack(unit):
    return int(unit[0]) + 2 * int(unit[1]) + 4 * (unit[2] == "M")


def select(key, table):
    out = jnp.int32(0)
    for k, v in table.items():
        out = jnp.where(key == k, jnp.int32(v), out)
    return out


def token_tables():
    count, what = {}, {}
    for r, role in enumerate(ROLES):
        for array in (DY, X):
            for g, units in enumerate(TOKENS[role][array]):
                for h in range(H):
                    if array == DY:
                        s = h if g == 0 else (g - 1) * H + h + H + 1
                    else:
                        s = X_FROM[role] + g * H + h
                    count[r * 100 + s] = len(units)
                    for k, unit in enumerate(units):
                        what[(r * 100 + s) * 10 + k] = pack(unit) + 8 * h + 16 * array
    return count, what


def sum_tables():
    count, what = {}, {}
    for r, role in enumerate(ROLES):
        for slot, entries in SUMS[role].items():
            count[r * 100 + slot] = len(entries)
            for k, (unit, links, out, before) in enumerate(entries):
                mask = sum(1 << link for link in links)
                code = pack(unit) + 8 * mask + 64 * (3 if out is None else out) + 256 * before
                what[(r * 100 + slot) * 10 + k] = code
    return count, what


def kernel(
    x, dy, gate, up, w_gate, w_up, w_down,
    dx, dw_gate, dw_up, dw_down, full, parts,
    wg, wu, wd, acc, dg, du, tok, gb, ub, dh, hid, total, ext, out, outw,
    ag_recv, ag_send, rs_recv, rs_send, w_send, w_sem, tok_sem, g_sem, u_sem, e_sem, st_sem,
):
    block, depth = dy.shape
    width = gate.shape[1]
    rows = block // H
    tile = 512
    own_in = {DY: dy, X: x}

    tp = lax.axis_index("tp")
    core, chip = tp % 2, tp // 2
    y, z = chip // 4, chip % 4
    half = z // 2
    middle = ((z + 1) % 4) // 2
    is_m, is_c = middle == 1, middle == 0
    role = 1 - middle

    def chip_of(yy, hh, mm):
        return yy * 4 + mm + hh * (3 - 2 * mm)

    def chip_at(unit):
        yy = 1 - y if unit[0] == "1" else y
        hh = 1 - half if unit[1] == "1" else half
        return chip_of(yy, hh, 1 if unit[2] == "M" else 0)

    def chip_packed(code):
        ry, rh, mm = code % 2, (code // 2) % 2, (code // 4) % 2
        return chip_of(y + ry - 2 * y * ry, half + rh - 2 * half * rh, mm)

    partner = tp + 1 - 2 * core
    at_link = {
        P_: chip_of(y, half, 1 - middle) * 2 + core,
        D_: chip_of(y, 1 - half, middle) * 2 + core,
        Y_: chip_of(1 - y, half, middle) * 2 + core,
        W_: partner,
    }

    def piece(h):
        return pl.ds(pl.multiple_of(h * rows, rows), rows)

    def remote(src, dst, send, recv, to):
        return pltpu.make_async_remote_copy(
            src_ref=src, dst_ref=dst, send_sem=send, recv_sem=recv, device_id={"tp": to}, device_id_type=MESH
        )


    def gather(link, array, unit, own, h):
        c = chip_at(unit)
        to = full.at[array, c * 2 + core, piece(h)]
        return remote(
            own_in[array].at[piece(h)] if own else to, to, ag_send.at[link, array, c, h], ag_recv.at[array, c * 2 + core, h],
            at_link[link],
        )

    def arrived(array, unit, h):
        c = chip_at(unit)
        to = full.at[array, c * 2 + core, piece(h)]
        remote(to, to, ag_send.at[W_, array, c, h], ag_recv.at[array, c * 2 + core, h], partner).wait_recv()

    def communicate(slot, name, h):
        for array, unit in RECEIVES[name].get(slot - 1, []):
            arrived(array, unit, h)
        for link in (P_, D_, Y_):
            entry = SENDS[name].get(link, {}).get(slot)
            if entry:
                gather(link, *entry, entry[1] == "00" + name, h).start()
        if slot in (0, 1):
            gather(W_, slot, "00" + name, True, h).start()
        for array, unit in RECEIVES[name].get(slot - 1, []):
            gather(W_, array, unit, False, h).start()


    sum_count, sum_what = sum_tables()

    def dx_term(index, plane):
        span = pl.ds(pl.multiple_of(plane * rows, rows), rows)

        def column(n, _):
            cols = pl.ds(pl.multiple_of(n * tile, tile), tile)
            total[:, cols] = lax.dot_general(
                dg[index, span, :], wg[cols, :], (((1,), (1,)), ((), ())), preferred_element_type=F32
            ) + lax.dot_general(du[index, span, :], wu[cols, :], (((1,), (1,)), ((), ())), preferred_element_type=F32)
            return 0

        lax.fori_loop(0, depth // tile, column, 0)

    def by_rows(step, n_rows, fn):
        def body(i, _):
            fn(pl.ds(pl.multiple_of(i * step, step), step))
            return 0

        lax.fori_loop(0, n_rows // step, body, 0)

    def term_in(kind, c, h):
        return pltpu.make_async_copy(parts.at[kind, c, piece(h)], ext.at[kind], e_sem.at[kind])

    def send_term(link, c, h, to):
        return remote(out.at[link, h], parts.at[link, c, piece(h)], rs_send.at[link, h], rs_recv.at[link, c, h], to)

    def reduce_one(code, h):
        c = chip_packed(code)
        mask, link, before = (code // 8) % 8, (code // 64) % 4, code // 256
        bits = [mask % 2 == 1, (mask // 2) % 2 == 1, mask // 4 == 1]
        for kind in (P_, D_, Y_, W_):

            def fetch(kind=kind):
                remote(ext.at[kind], parts.at[kind, c, piece(h)], w_send.at[0], rs_recv.at[kind, c, h], partner).wait_recv()
                term_in(kind, c, h).start()

            fetch() if kind == W_ else pl.when(bits[kind])(fetch)
        dx_term(c * H + h, core)
        for kind in (P_, D_, Y_):

            @pl.when(bits[kind])
            def _(kind=kind):
                term_in(kind, c, h).wait()

                def add(r):
                    total[r, :] += ext[kind, r, :].astype(F32)

                by_rows(16, rows, add)

        term_in(W_, c, h).wait()

        @pl.when(link == 3)
        def _():
            def finish(r):
                ext[P_, r, :] = (total[r, :] + ext[W_, r, :].astype(F32)).astype(BF16)

            by_rows(16, rows, finish)
            done = pltpu.make_async_copy(ext.at[P_], dx.at[piece(h)], e_sem.at[P_])
            done.start()
            done.wait()

        @pl.when(link != 3)
        def _():
            to = jnp.where(link == P_, at_link[P_], jnp.where(link == D_, at_link[D_], at_link[Y_]))

            @pl.when(before == 1)
            def _():
                send_term(link, c, h, to).wait_send()

            def round_(r):
                out[link, h, r, :] = (total[r, :] + ext[W_, r, :].astype(F32)).astype(BF16)

            by_rows(16, rows, round_)
            send_term(link, c, h, to).start()

    def term_to_partner(code, h, b):
        c = chip_packed(code)
        return remote(outw.at[b], parts.at[W_, c, piece(h)], w_send.at[b], rs_recv.at[W_, c, h], partner)

    def partner_one(key, k, h):
        code = select(key * 10 + k, sum_what)
        b = k % 2
        dx_term(chip_packed(code) * H + h, 1 - core)

        @pl.when(k >= 2)
        def _():
            term_to_partner(code, h, b).wait_send()

        def round_(r):
            outw[b, r, :] = total[r, :].astype(BF16)

        by_rows(16, rows, round_)
        term_to_partner(code, h, b).start()


    tok_count, tok_what = token_tables()
    nj, ni = depth // 128, width // 128

    def tok_in(code, b, start):
        c, h, array = chip_packed(code), (code // 8) % 2, code // 16
        mine = c == chip
        for plane in range(2):
            blk = c * 2 + plane
            dst = tok.at[b, plane * rows : (plane + 1) * rows]
            src = full.at[array, blk, piece(h)]
            sem = tok_sem.at[b, plane]
            spread = pl.ds(pl.multiple_of(blk * block + h * rows, rows), rows)
            g_in = pltpu.make_async_copy(gate.at[spread], gb.at[b, plane * rows : (plane + 1) * rows], g_sem.at[b, plane])
            u_in = pltpu.make_async_copy(up.at[spread], ub.at[b, plane * rows : (plane + 1) * rows], u_sem.at[b, plane])
            if not start:
                pltpu.make_async_copy(src, dst, sem).wait()

                @pl.when(array == DY)
                def _(g_in=g_in, u_in=u_in):
                    g_in.wait()
                    u_in.wait()

                continue

            @pl.when(array == DY)
            def _(g_in=g_in, u_in=u_in):
                g_in.start()
                u_in.start()

            local = mine & (core == plane)

            @pl.when(core != plane)
            def _(src=src, sem=sem, blk=blk):
                remote(src, src, w_send.at[0], ag_recv.at[array, blk, h], partner).wait_recv()

            @pl.when(jnp.logical_not(local))
            def _(src=src, dst=dst, sem=sem):
                pltpu.make_async_copy(src, dst, sem).start()

            for a in (DY, X):

                @pl.when(local & (array == a))
                def _(a=a, dst=dst, sem=sem):
                    pltpu.make_async_copy(own_in[a].at[piece(h)], dst, sem).start()

    def zero(i):
        def body(k, _):
            acc[i, k] = jnp.zeros((128, 128), F32)
            return 0

        lax.fori_loop(0, ni * nj, body, 0)

    def work_dy(code, b):
        index = chip_packed(code) * H + (code // 8) % 2
        dh[...] = lax.dot_general(tok[b], wd[...], (((1,), (1,)), ((), ())), preferred_element_type=F32)

        def pointwise(r):
            g, u, d = gb[b, r, :].astype(F32), ub[b, r, :].astype(F32), dh[r, :]
            g2 = g * g
            t = jnp.tanh(g * (0.7978845608028654 + (0.7978845608028654 * 0.044715) * g2))
            cdf = 0.5 + 0.5 * t
            act = g * cdf
            slope = cdf + (0.5 * g) * (1.0 - t * t) * (0.7978845608028654 + (3 * 0.7978845608028654 * 0.044715) * g2)
            du[index, r, :] = (d * act).astype(BF16)
            dg[index, r, :] = ((d * u) * slope).astype(BF16)
            hid[r, :] = (act * u).astype(BF16)

        by_rows(16, 2 * rows, pointwise)

        def column(n, _):
            cols = pl.ds(pl.multiple_of(n * tile, tile), tile)
            new = lax.dot_general(hid[...], tok[b, :, cols], (((0,), (0,)), ((), ())), preferred_element_type=F32)
            for i in range(ni):
                for j in range(tile // 128):
                    k = i * nj + n * (tile // 128) + j
                    acc[0, k] += new[i * 128 : (i + 1) * 128, j * 128 : (j + 1) * 128]
            return 0

        lax.fori_loop(0, depth // tile, column, 0)

    def work_x(code, b):
        index = chip_packed(code) * H + (code // 8) % 2

        def column(n, _):
            cols = pl.ds(pl.multiple_of(n * tile, tile), tile)
            xt = tok[b, :, cols]
            for a, d in enumerate((dg, du)):
                new = lax.dot_general(xt, d[index], (((0,), (0,)), ((), ())), preferred_element_type=F32)
                for i in range(tile // 128):
                    for j in range(ni):
                        k = (n * (tile // 128) + i) * ni + j
                        acc[a, k] += new[i * 128 : (i + 1) * 128, j * 128 : (j + 1) * 128]
            return 0

        lax.fori_loop(0, depth // tile, column, 0)

    def finish_down():
        for i in range(ni):
            b = i % 2
            put = pltpu.make_async_copy(tok.at[b, 0:128], dw_down.at[pl.ds(i * 128, 128)], st_sem.at[0, b])
            if i >= 2:
                put.wait()
            for j in range(nj):
                tok[b, 0:128, j * 128 : (j + 1) * 128] = acc[0, i * nj + j].astype(BF16)
            put.start()
        for i in range(max(ni - 2, 0), ni):
            pltpu.make_async_copy(tok.at[i % 2, 0:128], dw_down.at[pl.ds(i * 128, 128)], st_sem.at[0, i % 2]).wait()

    def finish_gate_up():
        def put(a, i, b):
            to = (dw_gate, dw_up)[a].at[pl.ds(pl.multiple_of(i * 128, 128), 128)]
            return pltpu.make_async_copy((gb, ub)[a].at[b, 0:128], to, st_sem.at[a, b])

        def body(i, _):
            b = i % 2
            for a in range(2):

                @pl.when(i >= 2)
                def _(a=a):
                    put(a, i, b).wait()

                for j in range(ni):
                    (gb, ub)[a][b, 0:128, j * 128 : (j + 1) * 128] = acc[a, i * ni + j].astype(BF16)
                put(a, i, b).start()
            return 0

        lax.fori_loop(0, nj, body, 0)
        for a in range(2):
            for b in range(2):
                put(a, 0, b).wait()


    loads = [pltpu.make_async_copy(s, d, w_sem.at[i]) for i, (s, d) in enumerate(((w_down, wd), (w_gate, wg), (w_up, wu)))]
    for load in loads:
        load.start()

    barrier = pltpu.get_barrier_semaphore()
    for link in (P_, Y_, W_):
        pl.semaphore_signal(barrier, inc=1, device_id={"tp": at_link[link]}, device_id_type=MESH)

    @pl.when(is_m)
    def _():
        pl.semaphore_signal(barrier, inc=1, device_id={"tp": at_link[D_]}, device_id_type=MESH)
        pl.semaphore_wait(barrier, 4)

    @pl.when(is_c)
    def _():
        pl.semaphore_wait(barrier, 3)

    zero(0)
    x_from = jnp.where(is_m, X_FROM["M"], X_FROM["C"])

    def step(s, _):
        slot, h = s // H, s % H
        for name, here in (("M", is_m), ("C", is_c)):
            for t in range(SLOTS):
                if t - 1 in RECEIVES[name] or any(t in v for v in SENDS[name].values()):

                    @pl.when(here & (slot == t))
                    def _(t=t, name=name):
                        communicate(t, name, h)

        @pl.when(s == x_from)
        def _():
            finish_down()
            zero(0)
            zero(1)

        key = role * 100 + s
        n_tok = select(key, tok_count)

        @pl.when(n_tok > 0)
        def _():
            tok_in(select(key * 10, tok_what), 0, True)

        @pl.when(s == 0)
        def _():
            for load in loads:
                load.wait()

        sum_key = role * 100 + slot

        def sums(k, _):
            reduce_one(select(sum_key * 10 + k, sum_what), h)
            return 0

        lax.fori_loop(0, select(sum_key, sum_count), sums, 0)

        def tokens(k, _):
            code, b = select(key * 10 + k, tok_what), k % 2

            @pl.when(k + 1 < n_tok)
            def _():
                tok_in(select(key * 10 + k + 1, tok_what), 1 - b, True)

            tok_in(code, b, False)

            @pl.when(code // 16 == DY)
            def _():
                work_dy(code, b)

            @pl.when(code // 16 == X)
            def _():
                work_x(code, b)

            return 0

        lax.fori_loop(0, n_tok, tokens, 0)

        next_key = role * 100 + (s + 1) // H
        next_h = (s + 1) % H
        n_next = select(next_key, sum_count)

        def partners(k, _):
            partner_one(next_key, k, next_h)
            return 0

        lax.fori_loop(0, n_next, partners, 0)
        for b in range(2):

            @pl.when(n_next > b)
            def _(b=b):
                term_to_partner(0, 0, b).wait_send()

        @pl.when(s == H * 9)
        def _():
            finish_gate_up()

        return 0

    lax.fori_loop(0, SLOTS * H, step, 0)

    for name, here in (("M", is_m), ("C", is_c)):

        @pl.when(here)
        def _(name=name):
            def drain(h, _):
                for link, entries in SENDS[name].items():
                    for array, unit in entries.values():
                        gather(link, array, unit, False, h).wait_send()
                for array in (DY, X):
                    gather(W_, array, "00" + name, False, h).wait_send()
                for entries in RECEIVES[name].values():
                    for array, unit in entries:
                        gather(W_, array, unit, False, h).wait_send()
                for link in {out_ for entries in SUMS[name].values() for _, _, out_, _ in entries if out_ is not None}:
                    send_term(link, chip, h, partner).wait_send()
                return 0

            lax.fori_loop(0, H, drain, 0)


def solution(mesh):
    def step(x, dy, gate, up, w_gate, w_up, w_down):
        block, depth = dy.shape
        tokens, width = gate.shape
        rows = block // H
        blocks = tokens // block
        anywhere = pl.BlockSpec(memory_space=pl.ANY)
        dma, flops = pltpu.SemaphoreType.DMA, 12 * tokens * depth * width
        outs = pl.pallas_call(
            kernel,
            out_shape=[
                jax.ShapeDtypeStruct((block, depth), BF16),
                jax.ShapeDtypeStruct((depth, width), BF16),
                jax.ShapeDtypeStruct((depth, width), BF16),
                jax.ShapeDtypeStruct((width, depth), BF16),
                jax.ShapeDtypeStruct((2, blocks, block, depth), BF16),
                jax.ShapeDtypeStruct((4, blocks // 2, block, depth), BF16),
            ],
            in_specs=[anywhere] * 7,
            out_specs=[anywhere] * 6,
            scratch_shapes=[
                pltpu.VMEM((depth, width), BF16),
                pltpu.VMEM((depth, width), BF16),
                pltpu.VMEM((width, depth), BF16),
                pltpu.VMEM((2, (depth // 128) * (width // 128), 128, 128), F32),
                pltpu.VMEM((blocks // 2 * H, 2 * rows, width), BF16),
                pltpu.VMEM((blocks // 2 * H, 2 * rows, width), BF16),
                pltpu.VMEM((2, 2 * rows, depth), BF16),
                pltpu.VMEM((2, 2 * rows, width), BF16),
                pltpu.VMEM((2, 2 * rows, width), BF16),
                pltpu.VMEM((2 * rows, width), F32),
                pltpu.VMEM((2 * rows, width), BF16),
                pltpu.VMEM((rows, depth), F32),
                pltpu.VMEM((4, rows, depth), BF16),
                pltpu.VMEM((3, H, rows, depth), BF16),
                pltpu.VMEM((2, rows, depth), BF16),
                dma((2, blocks, H)),
                dma((4, 2, blocks // 2, H)),
                dma((4, blocks // 2, H)),
                dma((3, H)),
                dma((2,)),
                dma((3,)),
                dma((2, 2)),
                dma((2, 2)),
                dma((2, 2)),
                dma((4,)),
                dma((2, 2)),
            ],
            compiler_params=pltpu.CompilerParams(collective_id=0, has_side_effects=True, vmem_limit_bytes=67043328),
            cost_estimate=pl.CostEstimate(flops=flops, bytes_accessed=12 * tokens * depth, transcendentals=tokens * width),
            name="mlp_backward",
        )(x, dy, gate, up, w_gate, w_up, w_down)
        return tuple(outs[:4])

    rows_, cols_ = P(("dp", "tp"), None), P("dp", "tp")
    return jax.shard_map(
        step,
        mesh=mesh,
        in_specs=(rows_, rows_, cols_, cols_, P(None, "tp"), P(None, "tp"), P("tp", None)),
        out_specs=(rows_, cols_, cols_, rows_),
        check_vma=False,
    )
```

time: 700 us -> 447 us (0.64)
  waiting for transfers between devices: 461 us -> 0 us
  Pallas kernels: 0 us -> 435 us
  matrix products: 218 us -> 0 us
  between operations: 13.8 us -> 0.65 us
    pallas_call x0 -> x1, Pallas kernels: none -> 435 us  [step(): pl.pallas_call(kernel, out_shape=[jax.ShapeDtypeStruct((block, depth), BF...]
    unnamed x5 -> x0, waiting for transfers between devices: 409 us -> none
    dot_general x6 -> x0, matrix products: 218 us -> none  [the longest x3 98.2 us: by_group(): jnp.einsum('gta,gtb->gab', a, b, preferred_element_type=jnp.float32)]
    reshape x1 -> x0, waiting for transfers between devices: 52 us -> none  [by_group(): a, b = (t.reshape(groups, -1, t.shape[-1]) for t in (a, b))]
  transfers between devices with their start and end apart: 3 -> 0, of which waited for: 3 -> 0; matrix products, arithmetic and copies ran while one was open for 32% -> 0% of each run, Pallas kernels for 0% -> 0%
where the time goes in v1:
time: 447 us
  Pallas kernels  435 us (97%)
  local copies, waits for them, and re-layouts  11.1 us (2%)
    pallas_call x1, Pallas kernels, step(): pl.pallas_call(kernel, out_shape=[jax.ShapeDtypeStruct((block, depth), BF...  435 us
    unnamed x10, local copies, waits for them, and re-layouts  11.1 us

profile of v1, /device:TPU:0, one launch (start us, length us, event | category | flops | bytes accessed | tf_op | source)
XLA Modules:
  0.0 446.7 jit_solution(4019829459966119981)
XLA Ops:
  0.6 434.9 %mlp_backward.1 = (bf16[416,2560]{1,0:T(8,128)(2,1)}, bf16[2560,640]{1,0:T(8,128)(2,1)}, bf16[2560,640]{1,0:T(8,128)(2,1)}, bf16[640,2560]{1,0:T(8,128)(2,1)}, b...) custom-call(bf16[416,2560]{1,0:T(8,128)(2,1)} %x.1, bf16[416,2560]{1,0:T(8,128)(2,1)} %dy.1, ...), custom_call_target="tpu_custom_call" | custom-call | flops 130862284800 | bytes 204472320 | tf_op jit(solution)/shard_map/mlp_backward/pallas_call | solution.py:535
  435.5 0.0 copy-start.2
  435.5 3.2 copy.15
  438.7 0.0 copy-done.2
  438.7 0.0 copy-start.1
  438.7 1.7 copy.16
  440.4 1.4 copy-done.1
  441.8 0.0 copy-start
  441.8 1.7 copy.17
  443.5 1.4 copy-done
  444.9 1.7 copy.18
Async XLA Ops:
  435.5 3.2 copy-start.2
  438.7 3.1 copy-start.1
  441.8 3.1 copy-start

commit v2 on v1

v2 whole, which is shorter than its diff:
```python
import jax
import jax.numpy as jnp
from jax import lax
from jax.experimental import pallas as pl
from jax.experimental.pallas import tpu as pltpu
from jax.sharding import PartitionSpec as P

MESH = pl.DeviceIdType.MESH
F32, BF16 = jnp.float32, jnp.bfloat16

P_, D_, Y_, W_ = 0, 1, 2, 3
DY, X = 0, 1
ROLES = "MC"
LINKS = {"a": ("C", "C", Y_), "b": ("M", "C", P_), "c": ("C", "M", P_), "d": ("M", "M", D_), "e": ("M", "M", Y_)}

START = {
    "a": {
        0: "d00C0", 2: "d00C1", 4: "d00M1", 6: "d01C1", 8: "d00M0", 10: "d01C0", 12: "d01M0", 14: "d01M1",
        16: "s10M0", 18: "x00M1", 20: "x00M0", 22: "x01C0", 24: "x01M0", 26: "x01C1", 28: "x00C1", 30: "s10M1",
        32: "x00C0",
    },
    "b": {
        0: "d00M1", 2: "d01M1", 4: "d01C1", 6: "d00M0", 8: "d01C0", 10: "d01M0", 12: "s10M0", 14: "x00M1",
        16: "x01M1", 18: "x00M0", 20: "x01C0", 22: "x01M0", 24: "x01C1", 26: "s10M1", 28: "x11M1", 30: "s00C0",
        32: "s00C1",
    },
    "c": {
        0: "d00C1", 2: "d00C0", 4: "x00C0", 6: "s10C0", 8: "s10C1", 10: "s01C1", 12: "s11C1", 14: "x00C1",
        16: "s01M0", 18: "s11C0", 20: "s11M0", 22: "s01C0", 24: "s00M0", 26: "s11M1", 28: "s01M1", 30: "x10C1",
        33: "s00M1",
    },
    "d": {
        0: "d00M1", 2: "d00C1", 4: "d10M0", 6: "d00C0", 8: "d00M0", 10: "x00M1", 12: "d10M1", 14: "s01C1",
        16: "s11C1", 18: "x00C0", 20: "x00M0", 22: "x00C1", 24: "x10M1", 26: "s01C0", 28: "s01M0", 30: "x10M0",
        33: "s01M1",
    },
    "e": {
        0: "d00M1", 2: "d00M0", 4: "d00C0", 6: "d00C1", 8: "d01C0", 10: "d01C1", 12: "s10C0", 14: "x00M1",
        16: "x00M0", 18: "x00C0", 20: "x01C0", 22: "s11C0", 24: "s11M0", 26: "x01C1", 28: "s10C1", 30: "s11M1",
    },
}
TOKENS = {
    "M": {
        0: ["d00M0"], 1: ["d00M1"], 4: ["d10M1", "d00C1"], 5: ["d01M1"],
        6: ["d10M0", "d01C1"], 7: ["d00C0"], 8: ["d10C0", "d11M0"], 10: ["d01C0", "d10C1"],
        12: ["d11C0", "d01M0"], 14: ["d11C1"], 16: ["d11M1"], 17: ["x00M1", "x00M0"],
        18: ["x00C0", "x01M1"], 19: ["x10M1", "x00C1"], 20: ["x10M0"], 22: ["x01C0", "x10C0"],
        24: ["x01M0", "x11C0"], 26: ["x01C1"], 28: ["x11M1"], 30: ["x11C1"],
        34: ["x10C1", "x11M0"],
    },
    "C": {
        0: ["d00C0"], 1: ["d00C1"], 4: ["d10C0", "d00M1"], 6: ["d10C1", "d01M1"],
        8: ["d01C1", "d10M1"], 10: ["d11C1", "d00M0"], 12: ["d10M0", "d01C0"], 14: ["d01M0", "d11C0"],
        16: ["d11M0"], 18: ["d11M1"], 19: ["x00C0", "x00C1"], 20: ["x00M1", "x01M1"],
        22: ["x10M1", "x00M0"], 24: ["x01C0", "x10M0"], 26: ["x01M0", "x11C0"], 28: ["x11M0", "x01C1"],
        30: ["x11C1"], 32: ["x11M1", "x10C1"], 36: ["x10C0"],
    },
}
X_FROM = {"M": 17, "C": 19}
LAST = {"M": (31, 36), "C": (33, 35)}
STEPS = 37
RING = 8


def seen_by_receiver(unit, link):
    flip = {"0": "1", "1": "0"}
    if link == Y_:
        return flip[unit[0]] + unit[1:]
    return unit[0] + flip[unit[1]] + unit[2] if link == D_ else unit


def pack(unit):
    return int(unit[0]) + 2 * int(unit[1]) + 4 * (unit[2] == "M")


def select(key, table):
    out = jnp.int32(0)
    for k, v in table.items():
        out = jnp.where(key == k, jnp.int32(v), out)
    return out


def plan():
    send, recv = ({P_: {}, D_: {}, Y_: {}} for _ in range(2))
    sums, terms = {"M": {}, "C": {}}, {}
    for name, entries in START.items():
        sender, receiver, link = LINKS[name]
        for n, (t, what) in enumerate(sorted(entries.items())):
            kind, unit, h = what[0], what[1:4], int(what[4])
            there = seen_by_receiver(unit, link)
            if kind == "s":
                count = sum(w[0] == "s" for s, w in entries.items() if s < t)
                sums[sender].setdefault(t, []).append((unit, h, link, count % 2, count >= 2))
                terms.setdefault((receiver, there, h), []).append(link)
                continue
            for k in range(2):
                code = 1 + "dx".index(kind) + 16 * (2 * h + k)
                send[link][ROLES.index(sender) * 100 + t + k] = code + 2 * pack(unit)
                recv[link][ROLES.index(receiver) * 100 + t + k + 2] = code + 2 * pack(there)
    for role in ROLES:
        for h in range(2):
            sums[role].setdefault(LAST[role][h], []).append(("00" + role, h, 3, 0, 0))
    sum_count, sum_what, tok_count, tok_what = {}, {}, {}, {}
    for r, role in enumerate(ROLES):
        for t, entries in sums[role].items():
            sum_count[r * 100 + t] = len(entries)
            for k, (unit, h, link, parity, before) in enumerate(entries):
                mask = sum(1 << i for i in terms.get((role, unit, h), []))
                sum_what[(r * 100 + t) * 10 + k] = pack(unit) + 8 * h + 16 * mask + 128 * link + 512 * parity + 1024 * before
        last = max(TOKENS[role])
        for t, entries in TOKENS[role].items():
            tok_count[r * 100 + t] = len(entries)
            for k, what in enumerate(entries):
                code = pack(what[1:4]) + 8 * int(what[4]) + 16 * "dx".index(what[0])
                tok_what[(r * 100 + t) * 10 + k] = code + 32 * (t == last and k == len(entries) - 1)
    return send, recv, sum_count, sum_what, tok_count, tok_what


def kernel(
    x, dy, gate, up, w_gate, w_up, w_down,
    dx, dw_gate, dw_up, dw_down, full, parts,
    wg, wu, wd, acc, dg, du, tok, gb, ub, dh, hid, total, ext, out, outw,
    ag_recv, ag_send, w_recv, w_send, rs_recv, rs_send, p_send, l_sem, tok_sem, g_sem, u_sem, e_sem, st_sem,
):
    block, depth = dy.shape
    width = gate.shape[1]
    rows, quarter = block // 2, block // 4
    tile = 512
    nj, ni = depth // 128, width // 128
    own_in = {DY: dy, X: x}
    send_what, recv_what, sum_count, sum_what, tok_count, tok_what = plan()

    tp = lax.axis_index("tp")
    core, chip = tp % 2, tp // 2
    y, z = chip // 4, chip % 4
    half = z // 2
    middle = ((z + 1) % 4) // 2
    is_m, is_c = middle == 1, middle == 0
    role = 1 - middle

    def chip_of(yy, hh, mm):
        return yy * 4 + mm + hh * (3 - 2 * mm)

    def chip_packed(code):
        ry, rh, mm = code % 2, (code // 2) % 2, (code // 4) % 2
        return chip_of(y + ry - 2 * y * ry, half + rh - 2 * half * rh, mm)

    partner = tp + 1 - 2 * core
    at_link = {
        P_: chip_of(y, half, 1 - middle) * 2 + core,
        D_: chip_of(y, 1 - half, middle) * 2 + core,
        Y_: chip_of(1 - y, half, middle) * 2 + core,
    }

    def span(h):
        return pl.ds(pl.multiple_of(h * rows, rows), rows)

    def remote(src, dst, send, recv, to):
        return pltpu.make_async_remote_copy(
            src_ref=src, dst_ref=dst, send_sem=send, recv_sem=recv, device_id={"tp": to}, device_id_type=MESH
        )

    def by_rows(step, n_rows, fn):
        def body(i, _):
            fn(pl.ds(pl.multiple_of(i * step, step), step))
            return 0

        lax.fori_loop(0, n_rows // step, body, 0)


    def on_link(link, code, s, src=None):
        code = code - 1
        array, c, p = code % 2, chip_packed(code // 2), code // 16
        piece = pl.ds(pl.multiple_of(p * quarter, quarter), quarter)
        to = full.at[array, c * 2 + core, piece]
        return remote(to if src is None else src.at[piece], to, ag_send.at[link, s % RING], ag_recv.at[array, c, p], at_link[link])

    def to_partner(array, c, h, src=None):
        to = full.at[array, c * 2 + core, span(h)]
        return remote(to if src is None else src.at[span(h)], to, w_send.at[array, c, h], w_recv.at[array, c, h], partner)

    def settle(s):
        for link in (P_, D_, Y_):

            @pl.when(select(role * 100 + s, send_what[link]) > 0)
            def _(link=link):
                on_link(link, jnp.int32(1), s).wait_send()

    def communicate(s):
        key = role * 100 + s
        come = {link: select(key, recv_what[link]) for link in (P_, D_, Y_)}
        for link, code in come.items():

            @pl.when(code > 0)
            def _(link=link, code=code):
                on_link(link, code, s).wait_recv()

        settle(s - RING)
        for link in (P_, D_, Y_):
            code = select(key, send_what[link])
            mine = chip_packed((code - 1) // 2) == chip

            @pl.when((code > 0) & jnp.logical_not(mine))
            def _(link=link, code=code):
                on_link(link, code, s).start()

            for array in (DY, X):

                @pl.when((code > 0) & mine & ((code - 1) % 2 == array))
                def _(link=link, code=code, array=array):
                    on_link(link, code, s, own_in[array]).start()

        for link, code in come.items():

            @pl.when((code > 0) & (((code - 1) // 16) % 2 == 1))
            def _(code=code):
                to_partner((code - 1) % 2, chip_packed((code - 1) // 2), (code - 1) // 32).start()

        for array, when in ((DY, 0), (X, 2)):

            @pl.when(s == when)
            def _(array=array):
                for h in range(2):
                    to_partner(array, chip, h, own_in[array]).start()


    def dx_term(code, plane):
        index = chip_packed(code) * 2 + (code // 8) % 2
        here = span(plane)

        def column(n, _):
            cols = pl.ds(pl.multiple_of(n * tile, tile), tile)
            total[:, cols] = lax.dot_general(
                dg[index, here, :], wg[cols, :], (((1,), (1,)), ((), ())), preferred_element_type=F32
            ) + lax.dot_general(du[index, here, :], wu[cols, :], (((1,), (1,)), ((), ())), preferred_element_type=F32)
            return 0

        lax.fori_loop(0, depth // tile, column, 0)

    def reduce_one(code):
        c, h = chip_packed(code), (code // 8) % 2
        mask, link, parity, before = (code // 16) % 8, (code // 128) % 4, (code // 512) % 2, code // 1024
        bits = {P_: mask % 2 == 1, D_: (mask // 2) % 2 == 1, Y_: mask // 4 == 1}

        def term_in(kind):
            return pltpu.make_async_copy(parts.at[kind, c, span(h)], ext.at[kind], e_sem.at[kind])

        def fetch(kind):
            remote(ext.at[kind], parts.at[kind, c, span(h)], p_send.at[0], rs_recv.at[kind, c, h], partner).wait_recv()
            term_in(kind).start()

        def send_term(to):
            return remote(out.at[link, parity], parts.at[link, c, span(h)], rs_send.at[link, parity], rs_recv.at[link, c, h], to)

        fetch(W_)
        for kind in (P_, D_, Y_):

            @pl.when(bits[kind] & (link != 3))
            def _(kind=kind):
                fetch(kind)

        dx_term(code, core)
        for kind in (P_, D_, Y_):

            @pl.when(bits[kind] & (link == 3))
            def _(kind=kind):
                fetch(kind)

        for kind in (P_, D_, Y_):

            @pl.when(bits[kind])
            def _(kind=kind):
                term_in(kind).wait()

                def add(r):
                    total[r, :] += ext[kind, r, :].astype(F32)

                by_rows(16, rows, add)

        term_in(W_).wait()

        @pl.when(link == 3)
        def _():
            def finish(r):
                ext[P_, r, :] = (total[r, :] + ext[W_, r, :].astype(F32)).astype(BF16)

            by_rows(16, rows, finish)
            done = pltpu.make_async_copy(ext.at[P_], dx.at[span(h)], e_sem.at[P_])
            done.start()
            done.wait()

        @pl.when(link != 3)
        def _():
            to = jnp.where(link == P_, at_link[P_], jnp.where(link == D_, at_link[D_], at_link[Y_]))

            @pl.when(before == 1)
            def _():
                send_term(to).wait_send()

            def round_(r):
                out[link, parity, r, :] = (total[r, :] + ext[W_, r, :].astype(F32)).astype(BF16)

            by_rows(16, rows, round_)
            send_term(to).start()

    def term_to_partner(code, b):
        c, h = chip_packed(code), (code // 8) % 2
        return remote(outw.at[b], parts.at[W_, c, span(h)], p_send.at[b], rs_recv.at[W_, c, h], partner)

    def partner_one(code, k):
        b = k % 2
        dx_term(code, 1 - core)

        @pl.when(k >= 2)
        def _():
            term_to_partner(code, b).wait_send()

        def round_(r):
            outw[b, r, :] = total[r, :].astype(BF16)

        by_rows(16, rows, round_)
        term_to_partner(code, b).start()


    def tok_in(code, b, start):
        c, h, array = chip_packed(code), (code // 8) % 2, (code // 16) % 2
        mine = c == chip
        for plane in range(2):
            blk = c * 2 + plane
            here = slice(plane * rows, (plane + 1) * rows)
            dst, src, sem = tok.at[b, here], full.at[array, blk, span(h)], tok_sem.at[b, plane]
            spread = pl.ds(pl.multiple_of(blk * block + h * rows, rows), rows)
            pair = (
                pltpu.make_async_copy(gate.at[spread], gb.at[b, here], g_sem.at[b, plane]),
                pltpu.make_async_copy(up.at[spread], ub.at[b, here], u_sem.at[b, plane]),
            )
            if not start:
                pltpu.make_async_copy(src, dst, sem).wait()

                @pl.when(array == DY)
                def _(pair=pair):
                    for copy in pair:
                        copy.wait()

                continue

            @pl.when(array == DY)
            def _(pair=pair):
                for copy in pair:
                    copy.start()

            local = mine & (core == plane)

            @pl.when(core != plane)
            def _(src=src):
                remote(src, src, p_send.at[0], w_recv.at[array, c, h], partner).wait_recv()

            @pl.when(jnp.logical_not(local))
            def _(src=src, dst=dst, sem=sem):
                pltpu.make_async_copy(src, dst, sem).start()

            for a in (DY, X):

                @pl.when(local & (array == a))
                def _(a=a, dst=dst, sem=sem):
                    pltpu.make_async_copy(own_in[a].at[span(h)], dst, sem).start()

    def work_dy(code, b):
        index = chip_packed(code) * 2 + (code // 8) % 2
        dh[...] = lax.dot_general(tok[b], wd[...], (((1,), (1,)), ((), ())), preferred_element_type=F32)

        def pointwise(r):
            g, u, d = gb[b, r, :].astype(F32), ub[b, r, :].astype(F32), dh[r, :]
            g2 = g * g
            t = jnp.tanh(g * (0.7978845608028654 + (0.7978845608028654 * 0.044715) * g2))
            cdf = 0.5 + 0.5 * t
            act = g * cdf
            slope = cdf + (0.5 * g) * (1.0 - t * t) * (0.7978845608028654 + (3 * 0.7978845608028654 * 0.044715) * g2)
            du[index, r, :] = (d * act).astype(BF16)
            dg[index, r, :] = ((d * u) * slope).astype(BF16)
            hid[r, :] = (act * u).astype(BF16)

        by_rows(16, 2 * rows, pointwise)

        def column(n, _):
            cols = pl.ds(pl.multiple_of(n * tile, tile), tile)
            new = lax.dot_general(hid[...], tok[b, :, cols], (((0,), (0,)), ((), ())), preferred_element_type=F32)
            for i in range(ni):
                for j in range(tile // 128):
                    k = i * nj + n * (tile // 128) + j
                    acc[0, k] += new[i * 128 : (i + 1) * 128, j * 128 : (j + 1) * 128]
            return 0

        lax.fori_loop(0, depth // tile, column, 0)

    places = 2 * (2 * rows // 128)

    def put(a, i):
        b = i % places
        here = (b // (places // 2), pl.ds(pl.multiple_of((b % (places // 2)) * 128, 128), 128))
        to = (dw_gate, dw_up)[a].at[pl.ds(pl.multiple_of(i * 128, 128), 128)]
        return here, pltpu.make_async_copy((gb, ub)[a].at[here], to, st_sem.at[a, b])

    def work_x(code, b):
        index = chip_packed(code) * 2 + (code // 8) % 2
        last = code // 32 == 1

        def column(n, _):
            cols = pl.ds(pl.multiple_of(n * tile, tile), tile)
            xt = tok[b, :, cols]
            for a, d in enumerate((dg, du)):
                new = lax.dot_general(xt, d[index], (((0,), (0,)), ((), ())), preferred_element_type=F32)
                for i in range(tile // 128):
                    for j in range(ni):
                        k = (n * (tile // 128) + i) * ni + j
                        acc[a, k] += new[i * 128 : (i + 1) * 128, j * 128 : (j + 1) * 128]

            @pl.when(last)
            def _():
                for i in range(tile // 128):
                    for a in range(2):
                        k = n * (tile // 128) + i
                        here, copy = put(a, k)

                        @pl.when(k >= places)
                        def _(copy=copy):
                            copy.wait()

                        for j in range(ni):
                            (gb, ub)[a][(*here, slice(j * 128, (j + 1) * 128))] = acc[a, k * ni + j].astype(BF16)
                        copy.start()

            return 0

        lax.fori_loop(0, depth // tile, column, 0)

        @pl.when(last)
        def _():
            for a in range(2):
                for i in range(max(nj - places, 0), nj):
                    put(a, i)[1].wait()

    def finish_down():
        copies = []
        for i in range(ni):
            at = (i * 128) // (2 * rows // 128 * 128)
            here = pl.ds(i * 128 - at * (2 * rows // 128 * 128), 128)
            copy = pltpu.make_async_copy(tok.at[at % 2, here], dw_down.at[pl.ds(i * 128, 128)], st_sem.at[0, at % 2 * (places // 2) + i % (places // 2)])
            if at >= 2:
                copies[i - places].wait()
            for j in range(nj):
                tok[at % 2, here, j * 128 : (j + 1) * 128] = acc[0, i * nj + j].astype(BF16)
                acc[0, i * nj + j] = jnp.zeros((128, 128), F32)
            copy.start()
            copies.append(copy)
        for copy in copies[max(ni - places, 0) :]:
            copy.wait()

    def clear(i):
        def body(k, _):
            acc[i, k] = jnp.zeros((128, 128), F32)
            return 0

        lax.fori_loop(0, ni * nj, body, 0)


    loads = [pltpu.make_async_copy(s, d, l_sem.at[i]) for i, (s, d) in enumerate(((w_down, wd), (w_gate, wg), (w_up, wu)))]
    for load in loads:
        load.start()

    barrier = pltpu.get_barrier_semaphore()
    for to in (at_link[P_], at_link[Y_], partner):
        pl.semaphore_signal(barrier, inc=1, device_id={"tp": to}, device_id_type=MESH)

    @pl.when(is_m)
    def _():
        pl.semaphore_signal(barrier, inc=1, device_id={"tp": at_link[D_]}, device_id_type=MESH)
        pl.semaphore_wait(barrier, 4)

    @pl.when(is_c)
    def _():
        pl.semaphore_wait(barrier, 3)

    x_from = jnp.where(is_m, X_FROM["M"], X_FROM["C"])

    def step(s, _):
        communicate(s)

        @pl.when(s == x_from)
        def _():
            finish_down()

        key = role * 100 + s
        n_tok = select(key, tok_count)

        @pl.when(n_tok > 0)
        def _():
            tok_in(select(key * 10, tok_what), 0, True)

        @pl.when(s == 0)
        def _():
            clear(0)
            clear(1)
            for load in loads:
                load.wait()

        def sums(k, _):
            reduce_one(select(key * 10 + k, sum_what))
            return 0

        lax.fori_loop(0, select(key, sum_count), sums, 0)

        def tokens(k, _):
            code, b = select(key * 10 + k, tok_what), k % 2

            @pl.when(k + 1 < n_tok)
            def _():
                tok_in(select(key * 10 + k + 1, tok_what), 1 - b, True)

            tok_in(code, b, False)

            @pl.when((code // 16) % 2 == DY)
            def _():
                work_dy(code, b)

            @pl.when((code // 16) % 2 == X)
            def _():
                work_x(code, b)

            return 0

        lax.fori_loop(0, n_tok, tokens, 0)

        n_next = select(key + 1, sum_count)

        def partners(k, _):
            partner_one(select((key + 1) * 10 + k, sum_what), k)
            return 0

        lax.fori_loop(0, n_next, partners, 0)
        for b in range(2):

            @pl.when(n_next > b)
            def _(b=b):
                term_to_partner(0, b).wait_send()

        return 0

    lax.fori_loop(0, STEPS, step, 0)

    def rest(s, _):
        settle(s)
        return 0

    lax.fori_loop(STEPS - RING, STEPS, rest, 0)
    for link in (P_, D_, Y_):

        @pl.when(is_m | (link != D_))
        def _(link=link):
            for parity in range(2):
                half_block = parts.at[link, 0, span(0)]
                remote(out.at[link, parity], half_block, rs_send.at[link, parity], rs_recv.at[link, 0, 0], partner).wait_send()

    def left(i, _):
        to_partner(i // 16, (i // 2) % 8, i % 2).wait_send()
        return 0

    lax.fori_loop(0, 32, left, 0)


def solution(mesh):
    def step(x, dy, gate, up, w_gate, w_up, w_down):
        block, depth = dy.shape
        tokens, width = gate.shape
        rows, chips = block // 2, tokens // block // 2
        places = 2 * (2 * rows // 128)
        anywhere = pl.BlockSpec(memory_space=pl.ANY)
        dma, flops = pltpu.SemaphoreType.DMA, 12 * tokens * depth * width
        outs = pl.pallas_call(
            kernel,
            out_shape=[
                jax.ShapeDtypeStruct((block, depth), BF16),
                jax.ShapeDtypeStruct((depth, width), BF16),
                jax.ShapeDtypeStruct((depth, width), BF16),
                jax.ShapeDtypeStruct((width, depth), BF16),
                jax.ShapeDtypeStruct((2, 2 * chips, block, depth), BF16),
                jax.ShapeDtypeStruct((4, chips, block, depth), BF16),
            ],
            in_specs=[anywhere] * 7,
            out_specs=[anywhere] * 6,
            scratch_shapes=[
                pltpu.VMEM((depth, width), BF16),
                pltpu.VMEM((depth, width), BF16),
                pltpu.VMEM((width, depth), BF16),
                pltpu.VMEM((2, (depth // 128) * (width // 128), 128, 128), F32),
                pltpu.VMEM((2 * chips, 2 * rows, width), BF16),
                pltpu.VMEM((2 * chips, 2 * rows, width), BF16),
                pltpu.VMEM((2, 2 * rows, depth), BF16),
                pltpu.VMEM((2, 2 * rows, width), BF16),
                pltpu.VMEM((2, 2 * rows, width), BF16),
                pltpu.VMEM((2 * rows, width), F32),
                pltpu.VMEM((2 * rows, width), BF16),
                pltpu.VMEM((rows, depth), F32),
                pltpu.VMEM((4, rows, depth), BF16),
                pltpu.VMEM((3, 2, rows, depth), BF16),
                pltpu.VMEM((2, rows, depth), BF16),
                dma((2, chips, 4)),
                dma((3, RING)),
                dma((2, chips, 2)),
                dma((2, chips, 2)),
                dma((4, chips, 2)),
                dma((3, 2)),
                dma((2,)),
                dma((3,)),
                dma((2, 2)),
                dma((2, 2)),
                dma((2, 2)),
                dma((4,)),
                dma((2, places)),
            ],
            compiler_params=pltpu.CompilerParams(collective_id=0, has_side_effects=True, vmem_limit_bytes=67043328),
            cost_estimate=pl.CostEstimate(flops=flops, bytes_accessed=12 * tokens * depth, transcendentals=tokens * width),
            name="mlp_backward",
        )(x, dy, gate, up, w_gate, w_up, w_down)
        return tuple(outs[:4])

    rows_, cols_ = P(("dp", "tp"), None), P("dp", "tp")
    return jax.shard_map(
        step,
        mesh=mesh,
        in_specs=(rows_, rows_, cols_, cols_, P(None, "tp"), P(None, "tp"), P("tp", None)),
        out_specs=(rows_, cols_, cols_, rows_),
        check_vma=False,
    )
```

time: 447 us -> 426 us (0.953)
  Pallas kernels: 435 us -> 414 us
    pallas_call x1, Pallas kernels: 435 us -> 414 us  [step(): pl.pallas_call(kernel, out_shape=[jax.ShapeDtypeStruct((block, depth), BF...]
where the time goes in v2:
time: 426 us; the launch traced here: 425 us
  Pallas kernels  414 us (97%)
  local copies, waits for them, and re-layouts  11.1 us (3%)
    pallas_call x1, Pallas kernels, step(): pl.pallas_call(kernel, out_shape=[jax.ShapeDtypeStruct((block, depth), BF...  414 us
    unnamed x10, local copies, waits for them, and re-layouts  11.1 us

profile of v2, /device:TPU:0, one launch (start us, length us, event | category | flops | bytes accessed | tf_op | source)
XLA Modules:
  0.0 425.3 jit_solution(9582084067329712142)
XLA Ops:
  0.6 413.5 %mlp_backward.1 = (bf16[416,2560]{1,0:T(8,128)(2,1)}, bf16[2560,640]{1,0:T(8,128)(2,1)}, bf16[2560,640]{1,0:T(8,128)(2,1)}, bf16[640,2560]{1,0:T(8,128)(2,1)}, b...) custom-call(bf16[416,2560]{1,0:T(8,128)(2,1)} %x.1, bf16[416,2560]{1,0:T(8,128)(2,1)} %dy.1, ...), custom_call_target="tpu_custom_call" | custom-call | flops 130862284800 | bytes 204472320 | tf_op jit(solution)/shard_map/mlp_backward/pallas_call | solution.py:579
  414.2 0.0 copy-start.2
  414.2 3.2 copy.15
  417.4 0.0 copy-done.2
  417.4 0.0 copy-start.1
  417.4 1.7 copy.16
  419.1 1.4 copy-done.1
  420.5 0.0 copy-start
  420.5 1.7 copy.17
  422.2 1.4 copy-done
  423.6 1.7 copy.18
Async XLA Ops:
  414.2 3.2 copy-start.2
  417.4 3.1 copy-start.1
  420.5 3.1 copy-start

commit v3 on v2

--- a/solution.py
+++ b/solution.py
@@ -14,50 +14,42 @@
 LINKS = {"a": ("C", "C", Y_), "b": ("M", "C", P_), "c": ("C", "M", P_), "d": ("M", "M", D_), "e": ("M", "M", Y_)}
 
 START = {
-    "a": {
-        0: "d00C0", 2: "d00C1", 4: "d00M1", 6: "d01C1", 8: "d00M0", 10: "d01C0", 12: "d01M0", 14: "d01M1",
-        16: "s10M0", 18: "x00M1", 20: "x00M0", 22: "x01C0", 24: "x01M0", 26: "x01C1", 28: "x00C1", 30: "s10M1",
-        32: "x00C0",
-    },
-    "b": {
-        0: "d00M1", 2: "d01M1", 4: "d01C1", 6: "d00M0", 8: "d01C0", 10: "d01M0", 12: "s10M0", 14: "x00M1",
-        16: "x01M1", 18: "x00M0", 20: "x01C0", 22: "x01M0", 24: "x01C1", 26: "s10M1", 28: "x11M1", 30: "s00C0",
-        32: "s00C1",
-    },
-    "c": {
-        0: "d00C1", 2: "d00C0", 4: "x00C0", 6: "s10C0", 8: "s10C1", 10: "s01C1", 12: "s11C1", 14: "x00C1",
-        16: "s01M0", 18: "s11C0", 20: "s11M0", 22: "s01C0", 24: "s00M0", 26: "s11M1", 28: "s01M1", 30: "x10C1",
-        33: "s00M1",
-    },
-    "d": {
-        0: "d00M1", 2: "d00C1", 4: "d10M0", 6: "d00C0", 8: "d00M0", 10: "x00M1", 12: "d10M1", 14: "s01C1",
-        16: "s11C1", 18: "x00C0", 20: "x00M0", 22: "x00C1", 24: "x10M1", 26: "s01C0", 28: "s01M0", 30: "x10M0",
-        33: "s01M1",
-    },
-    "e": {
-        0: "d00M1", 2: "d00M0", 4: "d00C0", 6: "d00C1", 8: "d01C0", 10: "d01C1", 12: "s10C0", 14: "x00M1",
-        16: "x00M0", 18: "x00C0", 20: "x01C0", 22: "s11C0", 24: "s11M0", 26: "x01C1", 28: "s10C1", 30: "s11M1",
-    },
+    "a": [
+        "d00C1", "d00M1", "d01M0", "d01C0", "d00C0", "d01C1", "d01M1", "d00M0", "x01C1", "x00C1", "x01M0", "x01M1",
+        "x01C0", "s10M0", "s10M1", "x00C0", "x00M1",
+    ],
+    "b": [
+        "d00M1", "d01M0", "d01C0", "s10M0", "d01C1", "d01M1", "d00M0", "x01C1", "s10M1", "x01M0", "x01M1", "x01C0",
+        "x00M1", "x10M0", "x00M0", "s00C0", "s00C1",
+    ],
+    "c": [
+        "d00C0", "d00C1", "x00C1", "s10C1", "x00C0", "s01C0", "s11M0", "s10C0", "s11C1", "s11C0", "x10C1", "s01C1",
+        "s11M1", "s01M0", "s01M1", "s00M0", "s00M1",
+    ],
+    "d": [
+        "d00M0", "d00C0", "d00C1", "d10M0", "d00M1", "d10M1", "x00C1", "s01C0", "x00M0", "x00M1", "x00C0", "s11C0",
+        "x10M1", "x10M0", "s01C1", "s01M0", "s01M1",
+    ],
+    "e": [
+        "d00M0", "d00M1", "d00C1", "d01C1", "d01C0", "s10C1", "d00C0", "x00M1", "s11M0", "x00C0", "s11C1", "x01C0",
+        "x00M0", "s10C0", "s11M1", "x01C1",
+    ],
 }
 TOKENS = {
-    "M": {
-        0: ["d00M0"], 1: ["d00M1"], 4: ["d10M1", "d00C1"], 5: ["d01M1"],
-        6: ["d10M0", "d01C1"], 7: ["d00C0"], 8: ["d10C0", "d11M0"], 10: ["d01C0", "d10C1"],
-        12: ["d11C0", "d01M0"], 14: ["d11C1"], 16: ["d11M1"], 17: ["x00M1", "x00M0"],
-        18: ["x00C0", "x01M1"], 19: ["x10M1", "x00C1"], 20: ["x10M0"], 22: ["x01C0", "x10C0"],
-        24: ["x01M0", "x11C0"], 26: ["x01C1"], 28: ["x11M1"], 30: ["x11C1"],
-        34: ["x10C1", "x11M0"],
-    },
-    "C": {
-        0: ["d00C0"], 1: ["d00C1"], 4: ["d10C0", "d00M1"], 6: ["d10C1", "d01M1"],
-        8: ["d01C1", "d10M1"], 10: ["d11C1", "d00M0"], 12: ["d10M0", "d01C0"], 14: ["d01M0", "d11C0"],
-        16: ["d11M0"], 18: ["d11M1"], 19: ["x00C0", "x00C1"], 20: ["x00M1", "x01M1"],
-        22: ["x10M1", "x00M0"], 24: ["x01C0", "x10M0"], 26: ["x01M0", "x11C0"], 28: ["x11M0", "x01C1"],
-        30: ["x11C1"], 32: ["x11M1", "x10C1"], 36: ["x10C0"],
-    },
+    "M": [
+        "0d00M0", "1d00M1", "4d10M0", "4d01M0", "5d00C0", "6d01C0", "6d10M1", "7d00C1", "8d10C1", "8d01C1", "10d11M0", "10d11C1",
+        "12d11C0", "12d01M1", "14d11M1", "16d10C0", "17x00M0", "17x00M1", "18x00C1", "18x00C0", "19x01C1", "19x10M1", "20x01M0", "22x10C0",
+        "22x01M1", "24x10C1", "24x01C0", "26x11C0", "28x10M0", "28x11M1", "30x11M0", "35x11C1",
+    ],
+    "C": [
+        "0d00C0", "1d00C1", "4d10C1", "4d00M1", "6d01M0", "6d10M1", "8d01C0", "8d11M0", "10d11C0", "12d10C0", "12d01C1", "14d11C1",
+        "14d01M1", "16d11M1", "16d00M0", "18d10M0", "19x00C0", "19x00C1", "20x01C1", "20x11C1", "22x10C1", "22x01M0", "24x11M0", "24x01M1",
+        "26x11M1", "26x01C0", "28x11C0", "28x00M1", "30x10M0", "32x00M0", "34x10C0", "36x10M1",
+    ],
 }
 X_FROM = {"M": 17, "C": 19}
-LAST = {"M": (31, 36), "C": (33, 35)}
+LAST = {"M": (33, 35), "C": (33, 35)}
+WAITS_LAST = {"M": True, "C": False}
 STEPS = 37
 RING = 8
 
@@ -85,42 +77,47 @@
     sums, terms = {"M": {}, "C": {}}, {}
     for name, entries in START.items():
         sender, receiver, link = LINKS[name]
-        for n, (t, what) in enumerate(sorted(entries.items())):
+        t = count = 0
+        for what in entries:
+            if what[0] == "+":
+                t += int(what)
+                continue
             kind, unit, h = what[0], what[1:4], int(what[4])
             there = seen_by_receiver(unit, link)
             if kind == "s":
-                count = sum(w[0] == "s" for s, w in entries.items() if s < t)
-                sums[sender].setdefault(t, []).append((unit, h, link, count % 2, count >= 2))
+                sums[sender].setdefault(t, []).append((unit, h, link, count % 2, count >= 2, 0))
                 terms.setdefault((receiver, there, h), []).append(link)
-                continue
-            for k in range(2):
+                count += 1
+            for k in range(0 if kind == "s" else 2):
                 code = 1 + "dx".index(kind) + 16 * (2 * h + k)
                 send[link][ROLES.index(sender) * 100 + t + k] = code + 2 * pack(unit)
                 recv[link][ROLES.index(receiver) * 100 + t + k + 2] = code + 2 * pack(there)
+            t += 2
     for role in ROLES:
         for h in range(2):
-            sums[role].setdefault(LAST[role][h], []).append(("00" + role, h, 3, 0, 0))
+            early = LAST[role][h] == max(LAST[role])
+            sums[role].setdefault(LAST[role][h], []).insert(0, ("00" + role, h, 3, 0, 0, early))
     sum_count, sum_what, tok_count, tok_what = {}, {}, {}, {}
     for r, role in enumerate(ROLES):
         for t, entries in sums[role].items():
             sum_count[r * 100 + t] = len(entries)
-            for k, (unit, h, link, parity, before) in enumerate(entries):
-                mask = sum(1 << i for i in terms.get((role, unit, h), []))
-                sum_what[(r * 100 + t) * 10 + k] = pack(unit) + 8 * h + 16 * mask + 128 * link + 512 * parity + 1024 * before
-        last = max(TOKENS[role])
-        for t, entries in TOKENS[role].items():
-            tok_count[r * 100 + t] = len(entries)
-            for k, what in enumerate(entries):
-                code = pack(what[1:4]) + 8 * int(what[4]) + 16 * "dx".index(what[0])
-                tok_what[(r * 100 + t) * 10 + k] = code + 32 * (t == last and k == len(entries) - 1)
+            for k, (unit, h, link, parity, before, early) in enumerate(entries):
+                code = pack(unit) + 8 * h + 16 * sum(1 << i for i in terms.get((role, unit, h), []))
+                sum_what[(r * 100 + t) * 10 + k] = code + 128 * link + 512 * parity + 1024 * before + 2048 * early
+        for what in TOKENS[role]:
+            t, kind, unit, h = int(what[:-5]), what[-5], what[-4:-1], int(what[-1])
+            k = tok_count.get(r * 100 + t, 0)
+            tok_count[r * 100 + t] = k + 1
+            code = pack(unit) + 8 * h + 16 * "dx".index(kind)
+            tok_what[(r * 100 + t) * 10 + k] = code + 32 * (what is TOKENS[role][-1])
     return send, recv, sum_count, sum_what, tok_count, tok_what
 
 
 def kernel(
     x, dy, gate, up, w_gate, w_up, w_down,
-    dx, dw_gate, dw_up, dw_down, full, parts,
-    wg, wu, wd, acc, dg, du, tok, gb, ub, dh, hid, total, ext, out, outw,
-    ag_recv, ag_send, w_recv, w_send, rs_recv, rs_send, p_send, l_sem, tok_sem, g_sem, u_sem, e_sem, st_sem,
+    dx, wg, wu, wd, full, parts,
+    acc, dg, du, tok, gb, ub, dh, hid, total, ext, out, outw,
+    ag_recv, ag_send, w_recv, w_send, rs_recv, rs_send, p_send, l_sem, tok_sem, g_sem, u_sem, e_sem,
 ):
     block, depth = dy.shape
     width = gate.shape[1]
@@ -239,7 +236,7 @@
 
     def reduce_one(code):
         c, h = chip_packed(code), (code // 8) % 2
-        mask, link, parity, before = (code // 16) % 8, (code // 128) % 4, (code // 512) % 2, code // 1024
+        mask, link, parity, before = (code // 16) % 8, (code // 128) % 4, (code // 512) % 2, (code // 1024) % 2
         bits = {P_: mask % 2 == 1, D_: (mask // 2) % 2 == 1, Y_: mask // 4 == 1}
 
         def term_in(kind):
@@ -259,7 +256,10 @@
             def _(kind=kind):
                 fetch(kind)
 
-        dx_term(code, core)
+        @pl.when(code < 2048)
+        def _():
+            dx_term(code, core)
+
         for kind in (P_, D_, Y_):
 
             @pl.when(bits[kind] & (link == 3))
@@ -282,12 +282,10 @@
         @pl.when(link == 3)
         def _():
             def finish(r):
-                ext[P_, r, :] = (total[r, :] + ext[W_, r, :].astype(F32)).astype(BF16)
+                to = pl.ds(pl.multiple_of(h * rows + r.start, 16), 16)
+                dx[to, :] = (total[r, :] + ext[W_, r, :].astype(F32)).astype(BF16)
 
             by_rows(16, rows, finish)
-            done = pltpu.make_async_copy(ext.at[P_], dx.at[span(h)], e_sem.at[P_])
-            done.start()
-            done.wait()
 
         @pl.when(link != 3)
         def _():
@@ -322,7 +320,22 @@
         term_to_partner(code, b).start()
 
 
+    def last_in(code, b, plane):
+        c, h = chip_packed(code), (code // 8) % 2
+        src = full.at[X, c * 2 + plane, span(h)]
+        return pltpu.make_async_copy(src, tok.at[b, span(plane)], tok_sem.at[b, plane])
+
     def tok_in(code, b, start):
+        @pl.when(code < 32)
+        def _():
+            pair_in(code, b, start)
+
+        @pl.when(code >= 32)
+        def _():
+            copy = last_in(code, b, core)
+            copy.start() if start else copy.wait()
+
+    def pair_in(code, b, start):
         c, h, array = chip_packed(code), (code // 8) % 2, (code // 16) % 2
         mine = c == chip
         for plane in range(2):
@@ -393,68 +406,43 @@
 
         lax.fori_loop(0, depth // tile, column, 0)
 
-    places = 2 * (2 * rows // 128)
-
-    def put(a, i):
-        b = i % places
-        here = (b // (places // 2), pl.ds(pl.multiple_of((b % (places // 2)) * 128, 128), 128))
-        to = (dw_gate, dw_up)[a].at[pl.ds(pl.multiple_of(i * 128, 128), 128)]
-        return here, pltpu.make_async_copy((gb, ub)[a].at[here], to, st_sem.at[a, b])
-
-    def work_x(code, b):
-        index = chip_packed(code) * 2 + (code // 8) % 2
-        last = code // 32 == 1
-
+    def x_columns(index, b, here, results):
         def column(n, _):
             cols = pl.ds(pl.multiple_of(n * tile, tile), tile)
-            xt = tok[b, :, cols]
+            xt = tok[b, here, cols]
             for a, d in enumerate((dg, du)):
-                new = lax.dot_general(xt, d[index], (((0,), (0,)), ((), ())), preferred_element_type=F32)
+                new = lax.dot_general(xt, d[index, here, :], (((0,), (0,)), ((), ())), preferred_element_type=F32)
                 for i in range(tile // 128):
                     for j in range(ni):
                         k = (n * (tile // 128) + i) * ni + j
-                        acc[a, k] += new[i * 128 : (i + 1) * 128, j * 128 : (j + 1) * 128]
-
-            @pl.when(last)
-            def _():
-                for i in range(tile // 128):
-                    for a in range(2):
-                        k = n * (tile // 128) + i
-                        here, copy = put(a, k)
-
-                        @pl.when(k >= places)
-                        def _(copy=copy):
-                            copy.wait()
-
-                        for j in range(ni):
-                            (gb, ub)[a][(*here, slice(j * 128, (j + 1) * 128))] = acc[a, k * ni + j].astype(BF16)
-                        copy.start()
-
+                        one = acc[a, k] + new[i * 128 : (i + 1) * 128, j * 128 : (j + 1) * 128]
+                        if results:
+                            to = pl.ds(pl.multiple_of(n * tile + i * 128, 128), 128)
+                            (wg, wu)[a][to, j * 128 : (j + 1) * 128] = one.astype(BF16)
+                        else:
+                            acc[a, k] = one
             return 0
 
         lax.fori_loop(0, depth // tile, column, 0)
 
-        @pl.when(last)
-        def _():
-            for a in range(2):
-                for i in range(max(nj - places, 0), nj):
-                    put(a, i)[1].wait()
+    def work_x(code, b):
+        x_columns(chip_packed(code) * 2 + (code // 8) % 2, b, slice(None), False)
+
+    def last_x(code, b):
+        c, h = chip_packed(code), (code // 8) % 2
+        x_columns(c * 2 + h, b, span(core), False)
+        there = full.at[X, c * 2 + 1 - core, span(h)]
+        remote(there, there, p_send.at[0], w_recv.at[X, c, h], partner).wait_recv()
+        copy = last_in(code, b, 1 - core)
+        copy.start()
+        copy.wait()
+        x_columns(c * 2 + h, b, span(1 - core), True)
 
     def finish_down():
-        copies = []
         for i in range(ni):
-            at = (i * 128) // (2 * rows // 128 * 128)
-            here = pl.ds(i * 128 - at * (2 * rows // 128 * 128), 128)
-            copy = pltpu.make_async_copy(tok.at[at % 2, here], dw_down.at[pl.ds(i * 128, 128)], st_sem.at[0, at % 2 * (places // 2) + i % (places // 2)])
-            if at >= 2:
-                copies[i - places].wait()
             for j in range(nj):
-                tok[at % 2, here, j * 128 : (j + 1) * 128] = acc[0, i * nj + j].astype(BF16)
+                wd[i * 128 : (i + 1) * 128, j * 128 : (j + 1) * 128] = acc[0, i * nj + j].astype(BF16)
                 acc[0, i * nj + j] = jnp.zeros((128, 128), F32)
-            copy.start()
-            copies.append(copy)
-        for copy in copies[max(ni - places, 0) :]:
-            copy.wait()
 
     def clear(i):
         def body(k, _):
@@ -483,7 +471,13 @@
 
     x_from = jnp.where(is_m, X_FROM["M"], X_FROM["C"])
 
+    last_sum = jnp.where(is_m, max(LAST["M"]), max(LAST["C"]))
+
     def step(s, _):
+        @pl.when(s == last_sum)
+        def _():
+            dx_term(select((role * 100 + s) * 10, sum_what), core)
+
         communicate(s)
 
         @pl.when(s == x_from)
@@ -508,8 +502,6 @@
             reduce_one(select(key * 10 + k, sum_what))
             return 0
 
-        lax.fori_loop(0, select(key, sum_count), sums, 0)
-
         def tokens(k, _):
             code, b = select(key * 10 + k, tok_what), k % 2
 
@@ -523,13 +515,26 @@
             def _():
                 work_dy(code, b)
 
-            @pl.when((code // 16) % 2 == X)
+            @pl.when(code // 16 == X)
             def _():
                 work_x(code, b)
 
-            return 0
-
-        lax.fori_loop(0, n_tok, tokens, 0)
+            @pl.when(code >= 32)
+            def _():
+                last_x(code, b)
+
+            return 0
+
+        n_sum = select(key, sum_count)
+        tokens_first = (s == last_sum) & jnp.where(is_m, WAITS_LAST["M"], WAITS_LAST["C"])
+
+        def phase(p, _):
+            now = (p == 0) != tokens_first
+            lax.fori_loop(0, jnp.where(now, n_sum, 0), sums, 0)
+            lax.fori_loop(0, jnp.where(now, 0, n_tok), tokens, 0)
+            return 0
+
+        lax.fori_loop(0, 2, phase, 0)
 
         n_next = select(key + 1, sum_count)
 
@@ -568,30 +573,40 @@
     lax.fori_loop(0, 32, left, 0)
 
 
+def store(*refs):
+    results, places, sem = refs[:4], refs[4:8], refs[8]
+    copies = []
+    for i, (result, place) in enumerate(zip(results, places)):
+        n = result.shape[0] // 4
+        for k in range(4):
+            here = pl.ds(k * n, n)
+            copies.append(pltpu.make_async_copy(result.at[here], place.at[here], sem.at[i, k]))
+    for copy in copies:
+        copy.start()
+    for copy in copies:
+        copy.wait()
+
+
 def solution(mesh):
     def step(x, dy, gate, up, w_gate, w_up, w_down):
         block, depth = dy.shape
         tokens, width = gate.shape
         rows, chips = block // 2, tokens // block // 2
-        places = 2 * (2 * rows // 128)
         anywhere = pl.BlockSpec(memory_space=pl.ANY)
         dma, flops = pltpu.SemaphoreType.DMA, 12 * tokens * depth * width
         outs = pl.pallas_call(
             kernel,
             out_shape=[
-                jax.ShapeDtypeStruct((block, depth), BF16),
-                jax.ShapeDtypeStruct((depth, width), BF16),
-                jax.ShapeDtypeStruct((depth, width), BF16),
-                jax.ShapeDtypeStruct((width, depth), BF16),
+                pltpu.VMEM((block, depth), BF16),
+                pltpu.VMEM((depth, width), BF16),
+                pltpu.VMEM((depth, width), BF16),
+                pltpu.VMEM((width, depth), BF16),
                 jax.ShapeDtypeStruct((2, 2 * chips, block, depth), BF16),
                 jax.ShapeDtypeStruct((4, chips, block, depth), BF16),
             ],
             in_specs=[anywhere] * 7,
-            out_specs=[anywhere] * 6,
+            out_specs=[pl.BlockSpec(memory_space=pltpu.VMEM)] * 4 + [anywhere] * 2,
             scratch_shapes=[
-                pltpu.VMEM((depth, width), BF16),
-                pltpu.VMEM((depth, width), BF16),
-                pltpu.VMEM((width, depth), BF16),
                 pltpu.VMEM((2, (depth // 128) * (width // 128), 128, 128), F32),
                 pltpu.VMEM((2 * chips, 2 * rows, width), BF16),
                 pltpu.VMEM((2 * chips, 2 * rows, width), BF16),
@@ -616,13 +631,21 @@
                 dma((2, 2)),
                 dma((2, 2)),
                 dma((4,)),
-                dma((2, places)),
             ],
-            compiler_params=pltpu.CompilerParams(collective_id=0, has_side_effects=True, vmem_limit_bytes=67043328),
+            compiler_params=pltpu.CompilerParams(collective_id=0, has_side_effects=True, vmem_limit_bytes=55050000),
             cost_estimate=pl.CostEstimate(flops=flops, bytes_accessed=12 * tokens * depth, transcendentals=tokens * width),
             name="mlp_backward",
         )(x, dy, gate, up, w_gate, w_up, w_down)
-        return tuple(outs[:4])
+        results = outs[:4]
+        return pl.pallas_call(
+            store,
+            out_shape=[jax.ShapeDtypeStruct(r.shape, BF16) for r in results],
+            in_specs=[pl.BlockSpec(memory_space=pltpu.VMEM)] * 4,
+            out_specs=[anywhere] * 4,
+            scratch_shapes=[dma((4, 4))],
+            compiler_params=pltpu.CompilerParams(vmem_limit_bytes=2**20),
+            name="store",
+        )(*results)
 
     rows_, cols_ = P(("dp", "tp"), None), P("dp", "tp")
     return jax.shard_map(

time: 426 us -> 420 us (0.986)
  local copies, waits for them, and re-layouts: 11.1 us -> 0 us
  Pallas kernels: 414 us -> 419 us
    unnamed x10 -> x0, local copies, waits for them, and re-layouts: 11.1 us -> none
    pallas_call x1 -> x2, Pallas kernels: 414 us -> 419 us  [the longest x1 414 us: step(): pl.pallas_call(kernel, out_shape=[pltpu.VMEM((block, depth), BF16), pltpu...]
where the time goes in v3:
time: 420 us; the launch traced here: 419 us
  Pallas kernels  419 us (100%)
    pallas_call x1, Pallas kernels, step(): pl.pallas_call(kernel, out_shape=[pltpu.VMEM((block, depth), BF16), pltpu...  414 us

profile of v3, /device:TPU:0, one launch (start us, length us, event | category | flops | bytes accessed | tf_op | source)
XLA Modules:
  0.0 419.3 jit_solution(11058772158698165867)
XLA Ops:
  0.6 414.2 %mlp_backward.1 = (bf16[416,2560]{1,0:T(8,128)(2,1)S(1)}, bf16[2560,640]{1,0:T(8,128)(2,1)S(1)}, bf16[2560,640]{1,0:T(8,128)(2,1)S(1)}, bf16[640,2560]{1,0:T(8,1...) custom-call(bf16[416,2560]{1,0:T(8,128)(2,1)} %x.1, bf16[416,2560]{1,0:T(8,128)(2,1)} %dy.1, ...), custom_call_target="tpu_custom_call" | custom-call | flops 130862284800 | bytes 204472320 | tf_op jit(solution)/shard_map/mlp_backward/pallas_call | solution.py:597
  414.8 4.5 %store.1 = (bf16[416,2560]{1,0:T(8,128)(2,1)}, bf16[2560,640]{1,0:T(8,128)(2,1)}, bf16[2560,640]{1,0:T(8,128)(2,1)}, bf16[640,2560]{1,0:T(8,128)(2,1)}) custom-call(bf16[416,2560]{1,0:T(8,128)(2,1)S(1)} %get-tuple-element.8.refs_0_, bf16[2560,640]{1,0:T(8,128)(2,1)S(1)} %get-tuple-element.9.refs_1_, bf16[2560,640]{1,0:T(8,128)(2,1)S(1)} %get-tuple-element.10.refs_2_, ...), custom_call_target="tpu_custom_call" | custom-call | tf_op jit(solution)/shard_map/store/pallas_call | solution.py:640

commit v4 on v3

--- a/solution.py
+++ b/solution.py
@@ -15,41 +15,40 @@
 
 START = {
     "a": [
-        "d00C1", "d00M1", "d01M0", "d01C0", "d00C0", "d01C1", "d01M1", "d00M0", "x01C1", "x00C1", "x01M0", "x01M1",
-        "x01C0", "s10M0", "s10M1", "x00C0", "x00M1",
+        "d00C0", "d00C1", "d00M0", "d01C0", "d01M0", "d01M1", "d00M1", "d01C1", "s10M0", "x01M1", "x00C0", "x00C1",
+        "x01C1", "x00M1", "s10M1", "x01M0", "x01C0",
     ],
     "b": [
-        "d00M1", "d01M0", "d01C0", "s10M0", "d01C1", "d01M1", "d00M0", "x01C1", "s10M1", "x01M0", "x01M1", "x01C0",
-        "x00M1", "x10M0", "x00M0", "s00C0", "s00C1",
+        "d00M0", "d01M0", "d01C0", "s10M0", "d01M1", "d00M1", "d01C1", "s10M1", "x01M1", "x10M0", "x01C0", "x01C1",
+        "x00M1", "x00M0", "x01M0", "s00C0", "s00C1",
     ],
     "c": [
-        "d00C0", "d00C1", "x00C1", "s10C1", "x00C0", "s01C0", "s11M0", "s10C0", "s11C1", "s11C0", "x10C1", "s01C1",
-        "s11M1", "s01M0", "s01M1", "s00M0", "s00M1",
+        "d00C0", "d00C1", "x00C0", "s10C0", "s10C1", "s01C0", "s11C0", "s01M0", "x00C1", "s01C1", "s11C1", "s11M0",
+        "x10C1", "s11M1", "s01M1", "s00M0", "s00M1",
     ],
     "d": [
-        "d00M0", "d00C0", "d00C1", "d10M0", "d00M1", "d10M1", "x00C1", "s01C0", "x00M0", "x00M1", "x00C0", "s11C0",
-        "x10M1", "x10M0", "s01C1", "s01M0", "s01M1",
+        "d00M0", "d00C0", "d10M0", "d00M1", "d10M1", "d00C1", "x00M0", "x00M1", "x10M0", "x00C0", "x00C1", "s01C1",
+        "s11C1", "s01C0", "x10M1", "s01M0", "+1", "s01M1",
     ],
     "e": [
-        "d00M0", "d00M1", "d00C1", "d01C1", "d01C0", "s10C1", "d00C0", "x00M1", "s11M0", "x00C0", "s11C1", "x01C0",
-        "x00M0", "s10C0", "s11M1", "x01C1",
+        "d00M0", "d00C0", "d00C1", "d00M1", "d01C0", "s10C0", "d01C1", "x00M0", "s11C0", "x00M1", "x01C0", "x01C1",
+        "x00C0", "s11M0", "s10C1", "s11M1",
     ],
 }
 TOKENS = {
     "M": [
-        "0d00M0", "1d00M1", "4d10M0", "4d01M0", "5d00C0", "6d01C0", "6d10M1", "7d00C1", "8d10C1", "8d01C1", "10d11M0", "10d11C1",
-        "12d11C0", "12d01M1", "14d11M1", "16d10C0", "17x00M0", "17x00M1", "18x00C1", "18x00C0", "19x01C1", "19x10M1", "20x01M0", "22x10C0",
-        "22x01M1", "24x10C1", "24x01C0", "26x11C0", "28x10M0", "28x11M1", "30x11M0", "35x11C1",
+        "0d00M0", "1d00M1", "4d10M0", "4d00C0", "5d01M0", "6d10C0", "6d01C0", "7d00C1", "8d11M0", "8d10C1", "10d10M1", "10d01M1",
+        "12d11C0", "12d11M1", "14d01C1", "16d11C1", "17x00M0", "17x00M1", "18x00C0", "18x01M0", "19x01M1", "19x10M0", "20x00C1", "20x11M0",
+        "22x10M1", "22x01C0", "24x01C1", "24x11C0", "26x11C1", "28x10C0", "28x10C1", "32x11M1",
     ],
     "C": [
-        "0d00C0", "1d00C1", "4d10C1", "4d00M1", "6d01M0", "6d10M1", "8d01C0", "8d11M0", "10d11C0", "12d10C0", "12d01C1", "14d11C1",
-        "14d01M1", "16d11M1", "16d00M0", "18d10M0", "19x00C0", "19x00C1", "20x01C1", "20x11C1", "22x10C1", "22x01M0", "24x11M0", "24x01M1",
-        "26x11M1", "26x01C0", "28x11C0", "28x00M1", "30x10M0", "32x00M0", "34x10C0", "36x10M1",
+        "0d00C0", "1d00C1", "4d10C0", "4d00M0", "6d10C1", "6d01M0", "8d01C0", "8d10M0", "10d11C0", "12d11M0", "12d01M1", "14d11M1",
+        "14d00M1", "16d01C1", "16d10M1", "18d11C1", "19x00C0", "19x00C1", "20x01M1", "22x11M1", "22x10M0", "24x10C0", "24x01C0", "26x01C1",
+        "26x10C1", "28x11C1", "28x00M1", "30x10M1", "30x00M0", "32x01M0", "34x11M0", "36x11C0",
     ],
 }
 X_FROM = {"M": 17, "C": 19}
-LAST = {"M": (33, 35), "C": (33, 35)}
-WAITS_LAST = {"M": True, "C": False}
+LAST = {"M": (33, 36), "C": (33, 35)}
 STEPS = 37
 RING = 8
 
@@ -113,10 +112,15 @@
     return send, recv, sum_count, sum_what, tok_count, tok_what
 
 
+def last_code(role):
+    what = TOKENS[role][-1]
+    return pack(what[-4:-1]) + 8 * int(what[-1])
+
+
 def kernel(
     x, dy, gate, up, w_gate, w_up, w_down,
-    dx, wg, wu, wd, full, parts,
-    acc, dg, du, tok, gb, ub, dh, hid, total, ext, out, outw,
+    dx, wd, acc, dg_last, du_last, full, parts,
+    wg, wu, dg, du, tok, gb, ub, dh, total, ext, out, outw,
     ag_recv, ag_send, w_recv, w_send, rs_recv, rs_send, p_send, l_sem, tok_sem, g_sem, u_sem, e_sem,
 ):
     block, depth = dy.shape
@@ -152,6 +156,9 @@
     def span(h):
         return pl.ds(pl.multiple_of(h * rows, rows), rows)
 
+    def quarter_at(p):
+        return pl.ds(pl.multiple_of(p * quarter, quarter), quarter)
+
     def remote(src, dst, send, recv, to):
         return pltpu.make_async_remote_copy(
             src_ref=src, dst_ref=dst, send_sem=send, recv_sem=recv, device_id={"tp": to}, device_id_type=MESH
@@ -168,13 +175,19 @@
     def on_link(link, code, s, src=None):
         code = code - 1
         array, c, p = code % 2, chip_packed(code // 2), code // 16
-        piece = pl.ds(pl.multiple_of(p * quarter, quarter), quarter)
+        piece = quarter_at(p)
         to = full.at[array, c * 2 + core, piece]
         return remote(to if src is None else src.at[piece], to, ag_send.at[link, s % RING], ag_recv.at[array, c, p], at_link[link])
 
-    def to_partner(array, c, h, src=None):
-        to = full.at[array, c * 2 + core, span(h)]
-        return remote(to if src is None else src.at[span(h)], to, w_send.at[array, c, h], w_recv.at[array, c, h], partner)
+    def to_partner(array, c, p, src=None):
+        piece = quarter_at(p)
+        to = full.at[array, c * 2 + core, piece]
+        return remote(to if src is None else src.at[piece], to, w_send.at[array, c, p], w_recv.at[array, c, p], partner)
+
+    def from_partner(array, c, h):
+        for k in range(2):
+            there = full.at[array, c * 2 + 1 - core, quarter_at(2 * h + k)]
+            remote(there, there, p_send.at[0], w_recv.at[array, c, 2 * h + k], partner).wait_recv()
 
     def settle(s):
         for link in (P_, D_, Y_):
@@ -209,16 +222,16 @@
 
         for link, code in come.items():
 
-            @pl.when((code > 0) & (((code - 1) // 16) % 2 == 1))
+            @pl.when(code > 0)
             def _(code=code):
-                to_partner((code - 1) % 2, chip_packed((code - 1) // 2), (code - 1) // 32).start()
+                to_partner((code - 1) % 2, chip_packed((code - 1) // 2), (code - 1) // 16).start()
 
         for array, when in ((DY, 0), (X, 2)):
 
             @pl.when(s == when)
             def _(array=array):
-                for h in range(2):
-                    to_partner(array, chip, h, own_in[array]).start()
+                for p in range(4):
+                    to_partner(array, chip, p, own_in[array]).start()
 
 
     def dx_term(code, plane):
@@ -320,10 +333,10 @@
         term_to_partner(code, b).start()
 
 
-    def last_in(code, b, plane):
+    def last_in(code, b):
         c, h = chip_packed(code), (code // 8) % 2
-        src = full.at[X, c * 2 + plane, span(h)]
-        return pltpu.make_async_copy(src, tok.at[b, span(plane)], tok_sem.at[b, plane])
+        src = full.at[X, c * 2 + core, span(h)]
+        return pltpu.make_async_copy(src, tok.at[b, span(core)], tok_sem.at[b, core])
 
     def tok_in(code, b, start):
         @pl.when(code < 32)
@@ -332,7 +345,7 @@
 
         @pl.when(code >= 32)
         def _():
-            copy = last_in(code, b, core)
+            copy = last_in(code, b)
             copy.start() if start else copy.wait()
 
     def pair_in(code, b, start):
@@ -365,8 +378,8 @@
             local = mine & (core == plane)
 
             @pl.when(core != plane)
-            def _(src=src):
-                remote(src, src, p_send.at[0], w_recv.at[array, c, h], partner).wait_recv()
+            def _():
+                from_partner(array, c, h)
 
             @pl.when(jnp.logical_not(local))
             def _(src=src, dst=dst, sem=sem):
@@ -391,13 +404,13 @@
             slope = cdf + (0.5 * g) * (1.0 - t * t) * (0.7978845608028654 + (3 * 0.7978845608028654 * 0.044715) * g2)
             du[index, r, :] = (d * act).astype(BF16)
             dg[index, r, :] = ((d * u) * slope).astype(BF16)
-            hid[r, :] = (act * u).astype(BF16)
+            gb[b, r, :] = (act * u).astype(BF16)
 
         by_rows(16, 2 * rows, pointwise)
 
         def column(n, _):
             cols = pl.ds(pl.multiple_of(n * tile, tile), tile)
-            new = lax.dot_general(hid[...], tok[b, :, cols], (((0,), (0,)), ((), ())), preferred_element_type=F32)
+            new = lax.dot_general(gb[b], tok[b, :, cols], (((0,), (0,)), ((), ())), preferred_element_type=F32)
             for i in range(ni):
                 for j in range(tile // 128):
                     k = i * nj + n * (tile // 128) + j
@@ -406,7 +419,7 @@
 
         lax.fori_loop(0, depth // tile, column, 0)
 
-    def x_columns(index, b, here, results):
+    def x_columns(index, b, here):
         def column(n, _):
             cols = pl.ds(pl.multiple_of(n * tile, tile), tile)
             xt = tok[b, here, cols]
@@ -415,28 +428,25 @@
                 for i in range(tile // 128):
                     for j in range(ni):
                         k = (n * (tile // 128) + i) * ni + j
-                        one = acc[a, k] + new[i * 128 : (i + 1) * 128, j * 128 : (j + 1) * 128]
-                        if results:
-                            to = pl.ds(pl.multiple_of(n * tile + i * 128, 128), 128)
-                            (wg, wu)[a][to, j * 128 : (j + 1) * 128] = one.astype(BF16)
-                        else:
-                            acc[a, k] = one
+                        acc[a, k] += new[i * 128 : (i + 1) * 128, j * 128 : (j + 1) * 128]
             return 0
 
         lax.fori_loop(0, depth // tile, column, 0)
 
     def work_x(code, b):
-        x_columns(chip_packed(code) * 2 + (code // 8) % 2, b, slice(None), False)
+        x_columns(chip_packed(code) * 2 + (code // 8) % 2, b, slice(None))
 
     def last_x(code, b):
         c, h = chip_packed(code), (code // 8) % 2
-        x_columns(c * 2 + h, b, span(core), False)
-        there = full.at[X, c * 2 + 1 - core, span(h)]
-        remote(there, there, p_send.at[0], w_recv.at[X, c, h], partner).wait_recv()
-        copy = last_in(code, b, 1 - core)
-        copy.start()
-        copy.wait()
-        x_columns(c * 2 + h, b, span(1 - core), True)
+        x_columns(c * 2 + h, b, span(core))
+
+        def keep(r):
+            there = pl.ds(pl.multiple_of((1 - core) * rows + r.start, 16), 16)
+            dg_last[r, :] = dg[c * 2 + h, there, :]
+            du_last[r, :] = du[c * 2 + h, there, :]
+
+        by_rows(16, rows, keep)
+        from_partner(X, c, h)
 
     def finish_down():
         for i in range(ni):
@@ -525,16 +535,8 @@
 
             return 0
 
-        n_sum = select(key, sum_count)
-        tokens_first = (s == last_sum) & jnp.where(is_m, WAITS_LAST["M"], WAITS_LAST["C"])
-
-        def phase(p, _):
-            now = (p == 0) != tokens_first
-            lax.fori_loop(0, jnp.where(now, n_sum, 0), sums, 0)
-            lax.fori_loop(0, jnp.where(now, 0, n_tok), tokens, 0)
-            return 0
-
-        lax.fori_loop(0, 2, phase, 0)
+        lax.fori_loop(0, select(key, sum_count), sums, 0)
+        lax.fori_loop(0, n_tok, tokens, 0)
 
         n_next = select(key + 1, sum_count)
 
@@ -567,24 +569,57 @@
                 remote(out.at[link, parity], half_block, rs_send.at[link, parity], rs_recv.at[link, 0, 0], partner).wait_send()
 
     def left(i, _):
-        to_partner(i // 16, (i // 2) % 8, i % 2).wait_send()
+        to_partner(i // 32, (i // 4) % 8, i % 4).wait_send()
         return 0
 
-    lax.fori_loop(0, 32, left, 0)
-
-
-def store(*refs):
-    results, places, sem = refs[:4], refs[4:8], refs[8]
+    lax.fori_loop(0, 64, left, 0)
+
+
+def finish(dx, wd, acc, dg, du, full, to_x, to_gate, to_up, to_down, rows_in, done, x_sem, d_sem, g_sem):
+    depth, width = to_gate.shape
+    rows, tile, ni = rows_in.shape[0], 512, width // 128
+    tp = lax.axis_index("tp")
+    core, y, z = tp % 2, tp // 8, (tp // 2) % 4
+    half, middle = z // 2, ((z + 1) % 4) // 2
+    code = jnp.where(middle == 1, last_code("M"), last_code("C"))
+    ry, rh, mm, h = code % 2, (code // 2) % 2, (code // 4) % 2, code // 8
+    yy, hh = y + ry - 2 * y * ry, half + rh - 2 * half * rh
+    chip = yy * 4 + mm + hh * (3 - 2 * mm)
+    load = pltpu.make_async_copy(full.at[X, chip * 2 + 1 - core, pl.ds(pl.multiple_of(h * rows, rows), rows)], rows_in, x_sem.at[0])
+    load.start()
     copies = []
-    for i, (result, place) in enumerate(zip(results, places)):
+    for i, (result, place) in enumerate(((dx, to_x), (wd, to_down))):
         n = result.shape[0] // 4
         for k in range(4):
             here = pl.ds(k * n, n)
-            copies.append(pltpu.make_async_copy(result.at[here], place.at[here], sem.at[i, k]))
+            copies.append(pltpu.make_async_copy(result.at[here], place.at[here], d_sem.at[i, k]))
     for copy in copies:
         copy.start()
+    load.wait()
+
+    def store(a, n):
+        here = pl.ds(pl.multiple_of(n * tile, tile), tile)
+        return pltpu.make_async_copy(done.at[a, here], (to_gate, to_up)[a].at[here], g_sem.at[a, n])
+
+    def column(n, _):
+        xt = rows_in[:, pl.ds(pl.multiple_of(n * tile, tile), tile)]
+        for a, d in enumerate((dg, du)):
+            new = lax.dot_general(xt, d[...], (((0,), (0,)), ((), ())), preferred_element_type=F32)
+            for i in range(tile // 128):
+                to = pl.ds(pl.multiple_of(n * tile + i * 128, 128), 128)
+                for j in range(ni):
+                    k = (n * (tile // 128) + i) * ni + j
+                    one = acc[a, k] + new[i * 128 : (i + 1) * 128, j * 128 : (j + 1) * 128]
+                    done[a, to, j * 128 : (j + 1) * 128] = one.astype(BF16)
+            store(a, n).start()
+        return 0
+
+    lax.fori_loop(0, depth // tile, column, 0)
     for copy in copies:
         copy.wait()
+    for n in range(depth // tile):
+        for a in range(2):
+            store(a, n).wait()
 
 
 def solution(mesh):
@@ -592,37 +627,38 @@
         block, depth = dy.shape
         tokens, width = gate.shape
         rows, chips = block // 2, tokens // block // 2
-        anywhere = pl.BlockSpec(memory_space=pl.ANY)
+        anywhere, inside = pl.BlockSpec(memory_space=pl.ANY), pl.BlockSpec(memory_space=pltpu.VMEM)
         dma, flops = pltpu.SemaphoreType.DMA, 12 * tokens * depth * width
         outs = pl.pallas_call(
             kernel,
             out_shape=[
                 pltpu.VMEM((block, depth), BF16),
-                pltpu.VMEM((depth, width), BF16),
-                pltpu.VMEM((depth, width), BF16),
                 pltpu.VMEM((width, depth), BF16),
+                pltpu.VMEM((2, (depth // 128) * (width // 128), 128, 128), F32),
+                pltpu.VMEM((rows, width), BF16),
+                pltpu.VMEM((rows, width), BF16),
                 jax.ShapeDtypeStruct((2, 2 * chips, block, depth), BF16),
                 jax.ShapeDtypeStruct((4, chips, block, depth), BF16),
             ],
             in_specs=[anywhere] * 7,
-            out_specs=[pl.BlockSpec(memory_space=pltpu.VMEM)] * 4 + [anywhere] * 2,
+            out_specs=[inside] * 5 + [anywhere] * 2,
             scratch_shapes=[
-                pltpu.VMEM((2, (depth // 128) * (width // 128), 128, 128), F32),
+                pltpu.VMEM((depth, width), BF16),
+                pltpu.VMEM((depth, width), BF16),
                 pltpu.VMEM((2 * chips, 2 * rows, width), BF16),
                 pltpu.VMEM((2 * chips, 2 * rows, width), BF16),
                 pltpu.VMEM((2, 2 * rows, depth), BF16),
                 pltpu.VMEM((2, 2 * rows, width), BF16),
                 pltpu.VMEM((2, 2 * rows, width), BF16),
                 pltpu.VMEM((2 * rows, width), F32),
-                pltpu.VMEM((2 * rows, width), BF16),
                 pltpu.VMEM((rows, depth), F32),
                 pltpu.VMEM((4, rows, depth), BF16),
                 pltpu.VMEM((3, 2, rows, depth), BF16),
                 pltpu.VMEM((2, rows, depth), BF16),
                 dma((2, chips, 4)),
                 dma((3, RING)),
-                dma((2, chips, 2)),
-                dma((2, chips, 2)),
+                dma((2, chips, 4)),
+                dma((2, chips, 4)),
                 dma((4, chips, 2)),
                 dma((3, 2)),
                 dma((2,)),
@@ -632,20 +668,25 @@
                 dma((2, 2)),
                 dma((4,)),
             ],
-            compiler_params=pltpu.CompilerParams(collective_id=0, has_side_effects=True, vmem_limit_bytes=55050000),
+            compiler_params=pltpu.CompilerParams(collective_id=0, has_side_effects=True, vmem_limit_bytes=47950000),
             cost_estimate=pl.CostEstimate(flops=flops, bytes_accessed=12 * tokens * depth, transcendentals=tokens * width),
             name="mlp_backward",
         )(x, dy, gate, up, w_gate, w_up, w_down)
-        results = outs[:4]
         return pl.pallas_call(
-            store,
-            out_shape=[jax.ShapeDtypeStruct(r.shape, BF16) for r in results],
-            in_specs=[pl.BlockSpec(memory_space=pltpu.VMEM)] * 4,
+            finish,
+            out_shape=[jax.ShapeDtypeStruct(a.shape, BF16) for a in (dy, w_gate, w_up, w_down)],
+            in_specs=[inside] * 5 + [anywhere],
             out_specs=[anywhere] * 4,
-            scratch_shapes=[dma((4, 4))],
-            compiler_params=pltpu.CompilerParams(vmem_limit_bytes=2**20),
-            name="store",
-        )(*results)
+            scratch_shapes=[
+                pltpu.VMEM((rows, depth), BF16),
+                pltpu.VMEM((2, depth, width), BF16),
+                dma((1,)),
+                dma((2, 4)),
+                dma((2, depth // 512)),
+            ],
+            compiler_params=pltpu.CompilerParams(vmem_limit_bytes=2**24),
+            name="finish",
+        )(*outs[:6])
 
     rows_, cols_ = P(("dp", "tp"), None), P("dp", "tp")
     return jax.shard_map(

time: 420 us -> 418 us (level)
    pallas_call x1, Pallas kernels: 414 us -> 410 us  [step(): pl.pallas_call(kernel, out_shape=[pltpu.VMEM((block, depth), BF16), pltpu...]
where the time goes in v4:
time: 418 us; the launch traced here: 417 us
  Pallas kernels  417 us (100%)
    pallas_call x1, Pallas kernels, step(): pl.pallas_call(kernel, out_shape=[pltpu.VMEM((block, depth), BF16), pltpu...  410 us

profile of v4, /device:TPU:0, one launch (start us, length us, event | category | flops | bytes accessed | tf_op | source)
XLA Modules:
  0.0 417.2 jit_solution(3298203768944341130)
XLA Ops:
  0.6 409.9 %mlp_backward.1 = (bf16[416,2560]{1,0:T(8,128)(2,1)S(1)}, bf16[640,2560]{1,0:T(8,128)(2,1)S(1)}, f32[2,100,128,128]{3,2,1,0:T(8,128)S(1)}, bf16[208,640]{1,0:T(8...) custom-call(bf16[416,2560]{1,0:T(8,128)(2,1)} %x.1, ...), custom_call_target="tpu_custom_call" | custom-call | flops 130862284800 | bytes 204472320 | tf_op jit(solution)/shard_map/mlp_backward/pallas_call | solution.py:632
  410.6 6.7 %finish.1 = (bf16[416,2560]{1,0:T(8,128)(2,1)}, bf16[2560,640]{1,0:T(8,128)(2,1)}, bf16[2560,640]{1,0:T(8,128)(2,1)}, bf16[640,2560]{1,0:T(8,128)(2,1)}) custom-call(bf16[416,2560]{1,0:T(8,128)(2,1)S(1)} %get-tuple-element.10.dx, bf16[640,2560]{1,0:T(8,128)(2,1)S(1)} %get-tuple-element.11.wd, f32[2,100,128,128]{3,2,1,0:T(8,128)S(1)} %get-tuple-element.12.acc, ...), custom_call_target="tpu_custom_call" | custom-call | tf_op jit(solution)/shard_map/finish/pallas_call | solution.py:675

commit v5 on v4

--- a/solution.py
+++ b/solution.py
@@ -15,42 +15,41 @@
 
 START = {
     "a": [
-        "d00C0", "d00C1", "d00M0", "d01C0", "d01M0", "d01M1", "d00M1", "d01C1", "s10M0", "x01M1", "x00C0", "x00C1",
-        "x01C1", "x00M1", "s10M1", "x01M0", "x01C0",
+        "d00C0", "x00C0", "d01M1", "d01C0", "d00M1", "d01C1", "d01M0", "d00C1", "d00M0", "s10M1", "x00C1", "x01C1",
+        "x00M0", "x01C0", "s10M0", "x01M0", "x01M1",
     ],
     "b": [
-        "d00M0", "d01M0", "d01C0", "s10M0", "d01M1", "d00M1", "d01C1", "s10M1", "x01M1", "x10M0", "x01C0", "x01C1",
-        "x00M1", "x00M0", "x01M0", "s00C0", "s00C1",
+        "d00M1", "d01M1", "d01C0", "d00M0", "d01C1", "d01M0", "x00M1", "s10M1", "x01M1", "s10M0", "x01C1", "x00M0",
+        "x01C0", "x10M1", "x01M0", "s00C1", "s00C0",
     ],
     "c": [
-        "d00C0", "d00C1", "x00C0", "s10C0", "s10C1", "s01C0", "s11C0", "s01M0", "x00C1", "s01C1", "s11C1", "s11M0",
-        "x10C1", "s11M1", "s01M1", "s00M0", "s00M1",
+        "d00C0", "x00C1", "d00C1", "s10C0", "x00C0", "s11M1", "s11C0", "s01C1", "s11C1", "s01M0", "s10C1", "s11M0",
+        "s01C0", "s01M1", "s00M1", "x10C1", "s00M0",
     ],
     "d": [
-        "d00M0", "d00C0", "d10M0", "d00M1", "d10M1", "d00C1", "x00M0", "x00M1", "x10M0", "x00C0", "x00C1", "s01C1",
-        "s11C1", "s01C0", "x10M1", "s01M0", "+1", "s01M1",
+        "d00M1", "d00C0", "x10M0", "d00C1", "d00M0", "d10M1", "x00C1", "x00M1", "d10M0", "s01C1", "s11C1", "x00C0",
+        "x10M1", "x00M0", "s01C0", "s01M1", "s01M0",
     ],
     "e": [
-        "d00M0", "d00C0", "d00C1", "d00M1", "d01C0", "s10C0", "d01C1", "x00M0", "s11C0", "x00M1", "x01C0", "x01C1",
-        "x00C0", "s11M0", "s10C1", "s11M1",
+        "x00M0", "d00C0", "d01C0", "d00C1", "d00M1", "d01C1", "d00M0", "x01C1", "s11C0", "s11M1", "s10C0", "x00M1",
+        "x01C0", "s10C1", "s11M0", "x00C0",
     ],
 }
 TOKENS = {
     "M": [
-        "0d00M0", "1d00M1", "4d10M0", "4d00C0", "5d01M0", "6d10C0", "6d01C0", "7d00C1", "8d11M0", "8d10C1", "10d10M1", "10d01M1",
-        "12d11C0", "12d11M1", "14d01C1", "16d11C1", "17x00M0", "17x00M1", "18x00C0", "18x01M0", "19x01M1", "19x10M0", "20x00C1", "20x11M0",
-        "22x10M1", "22x01C0", "24x01C1", "24x11C0", "26x11C1", "28x10C0", "28x10C1", "32x11M1",
+        "0d00M0", "1d00M1", "4d01M1", "4d00C0", "6d10C0", "6d01C0", "8d11C0", "8d00C1", "10d01C1", "10d10C1", "12d10M1", "12d01M0",
+        "14d11M1", "14d11C1", "16d10M0", "20d11M0", "21x00M0", "21x00M1", "22x10M0", "22x00C1", "23x11M0", "23x00C0", "24x01C1", "24x01M1",
+        "25x11C1", "26x01C0", "26x10M1", "28x11C0", "28x11M1", "30x01M0", "34x10C1", "34x10C0",
     ],
     "C": [
-        "0d00C0", "1d00C1", "4d10C0", "4d00M0", "6d10C1", "6d01M0", "8d01C0", "8d10M0", "10d11C0", "12d11M0", "12d01M1", "14d11M1",
-        "14d00M1", "16d01C1", "16d10M1", "18d11C1", "19x00C0", "19x00C1", "20x01M1", "22x11M1", "22x10M0", "24x10C0", "24x01C0", "26x01C1",
-        "26x10C1", "28x11C1", "28x00M1", "30x10M1", "30x00M0", "32x01M0", "34x11M0", "36x11C0",
+        "0d00C0", "1d00C1", "4d10C0", "4d00M1", "6d01M1", "8d11M1", "8d01C0", "10d11C0", "10d00M0", "12d01C1", "12d10M1", "14d11C1",
+        "14d01M0", "16d11M0", "18d10C1", "20d10M0", "21x00C0", "21x00C1", "22x10C0", "22x00M1", "23x01M1", "24x10C1", "24x01C1", "26x00M0",
+        "26x11C1", "28x01C0", "28x10M0", "30x10M1", "30x11C0", "32x01M0", "34x11M0", "36x11M1",
     ],
 }
-X_FROM = {"M": 17, "C": 19}
-LAST = {"M": (33, 36), "C": (33, 35)}
+X_FROM = {"M": 21, "C": 21}
+LAST = {"M": (35, 33), "C": (35, 33)}
 STEPS = 37
-RING = 8
 
 
 def seen_by_receiver(unit, link):
@@ -94,7 +93,7 @@
             t += 2
     for role in ROLES:
         for h in range(2):
-            early = LAST[role][h] == max(LAST[role])
+            early = h == (LAST[role][1] >= LAST[role][0])
             sums[role].setdefault(LAST[role][h], []).insert(0, ("00" + role, h, 3, 0, 0, early))
     sum_count, sum_what, tok_count, tok_what = {}, {}, {}, {}
     for r, role in enumerate(ROLES):
@@ -119,9 +118,9 @@
 
 def kernel(
     x, dy, gate, up, w_gate, w_up, w_down,
-    dx, wd, acc, dg_last, du_last, full, parts,
-    wg, wu, dg, du, tok, gb, ub, dh, total, ext, out, outw,
-    ag_recv, ag_send, w_recv, w_send, rs_recv, rs_send, p_send, l_sem, tok_sem, g_sem, u_sem, e_sem,
+    dx, wd, acc, d_last, last_rows, full, parts,
+    w, d, tok, gb, ub, dh, total, ext, out, outw,
+    ag_recv, ag_send, w_recv, w_send, rs_recv, rs_send, p_send, l_send, l_sem, tok_sem, g_sem, u_sem, e_sem,
 ):
     block, depth = dy.shape
     width = gate.shape[1]
@@ -172,29 +171,29 @@
         lax.fori_loop(0, n_rows // step, body, 0)
 
 
-    def on_link(link, code, s, src=None):
+    def on_link(link, code, src=None):
         code = code - 1
         array, c, p = code % 2, chip_packed(code // 2), code // 16
         piece = quarter_at(p)
         to = full.at[array, c * 2 + core, piece]
-        return remote(to if src is None else src.at[piece], to, ag_send.at[link, s % RING], ag_recv.at[array, c, p], at_link[link])
+        return remote(to if src is None else src.at[piece], to, ag_send.at[link], ag_recv.at[array, c, p], at_link[link])
 
     def to_partner(array, c, p, src=None):
         piece = quarter_at(p)
         to = full.at[array, c * 2 + core, piece]
-        return remote(to if src is None else src.at[piece], to, w_send.at[array, c, p], w_recv.at[array, c, p], partner)
+        return remote(to if src is None else src.at[piece], to, w_send.at[array], w_recv.at[array, c, p], partner)
+
+    last = jnp.where(is_m, last_code("M"), last_code("C"))
+
+    def last_to_partner():
+        c, h = chip_packed(last), last // 8
+        here = full.at[X, c * 2 + core, span(h)]
+        return remote(here, last_rows, l_send, w_recv.at[X, c, 2 * h + 1], partner)
 
     def from_partner(array, c, h):
         for k in range(2):
             there = full.at[array, c * 2 + 1 - core, quarter_at(2 * h + k)]
-            remote(there, there, p_send.at[0], w_recv.at[array, c, 2 * h + k], partner).wait_recv()
-
-    def settle(s):
-        for link in (P_, D_, Y_):
-
-            @pl.when(select(role * 100 + s, send_what[link]) > 0)
-            def _(link=link):
-                on_link(link, jnp.int32(1), s).wait_send()
+            remote(there, there, p_send, w_recv.at[array, c, 2 * h + k], partner).wait_recv()
 
     def communicate(s):
         key = role * 100 + s
@@ -203,28 +202,33 @@
 
             @pl.when(code > 0)
             def _(link=link, code=code):
-                on_link(link, code, s).wait_recv()
-
-        settle(s - RING)
+                on_link(link, code).wait_recv()
+
         for link in (P_, D_, Y_):
             code = select(key, send_what[link])
             mine = chip_packed((code - 1) // 2) == chip
 
             @pl.when((code > 0) & jnp.logical_not(mine))
             def _(link=link, code=code):
-                on_link(link, code, s).start()
+                on_link(link, code).start()
 
             for array in (DY, X):
 
                 @pl.when((code > 0) & mine & ((code - 1) % 2 == array))
                 def _(link=link, code=code, array=array):
-                    on_link(link, code, s, own_in[array]).start()
+                    on_link(link, code, own_in[array]).start()
 
         for link, code in come.items():
 
-            @pl.when(code > 0)
+            ends = ((code - 1) % 16 == X + 2 * (last % 8)) & ((code - 1) // 32 == last // 8)
+
+            @pl.when((code > 0) & jnp.logical_not(ends))
             def _(code=code):
                 to_partner((code - 1) % 2, chip_packed((code - 1) // 2), (code - 1) // 16).start()
+
+            @pl.when(ends & ((code - 1) // 16 % 2 == 1))
+            def _():
+                last_to_partner().start()
 
         for array, when in ((DY, 0), (X, 2)):
 
@@ -241,8 +245,8 @@
         def column(n, _):
             cols = pl.ds(pl.multiple_of(n * tile, tile), tile)
             total[:, cols] = lax.dot_general(
-                dg[index, here, :], wg[cols, :], (((1,), (1,)), ((), ())), preferred_element_type=F32
-            ) + lax.dot_general(du[index, here, :], wu[cols, :], (((1,), (1,)), ((), ())), preferred_element_type=F32)
+                d[index, here, :], w[cols, :], (((1,), (1,)), ((), ())), preferred_element_type=F32
+            )
             return 0
 
         lax.fori_loop(0, depth // tile, column, 0)
@@ -256,7 +260,7 @@
             return pltpu.make_async_copy(parts.at[kind, c, span(h)], ext.at[kind], e_sem.at[kind])
 
         def fetch(kind):
-            remote(ext.at[kind], parts.at[kind, c, span(h)], p_send.at[0], rs_recv.at[kind, c, h], partner).wait_recv()
+            remote(ext.at[kind], parts.at[kind, c, span(h)], p_send, rs_recv.at[kind, c, h], partner).wait_recv()
             term_in(kind).start()
 
         def send_term(to):
@@ -314,23 +318,22 @@
             by_rows(16, rows, round_)
             send_term(to).start()
 
-    def term_to_partner(code, b):
+    def term_to_partner(code):
         c, h = chip_packed(code), (code // 8) % 2
-        return remote(outw.at[b], parts.at[W_, c, span(h)], p_send.at[b], rs_recv.at[W_, c, h], partner)
-
-    def partner_one(code, k):
-        b = k % 2
+        return remote(outw, parts.at[W_, c, span(h)], p_send, rs_recv.at[W_, c, h], partner)
+
+    def partner_one(code, first):
         dx_term(code, 1 - core)
 
-        @pl.when(k >= 2)
-        def _():
-            term_to_partner(code, b).wait_send()
+        @pl.when(jnp.logical_not(first))
+        def _():
+            term_to_partner(code).wait_send()
 
         def round_(r):
-            outw[b, r, :] = total[r, :].astype(BF16)
+            outw[r, :] = total[r, :].astype(BF16)
 
         by_rows(16, rows, round_)
-        term_to_partner(code, b).start()
+        term_to_partner(code).start()
 
 
     def last_in(code, b):
@@ -396,14 +399,14 @@
         dh[...] = lax.dot_general(tok[b], wd[...], (((1,), (1,)), ((), ())), preferred_element_type=F32)
 
         def pointwise(r):
-            g, u, d = gb[b, r, :].astype(F32), ub[b, r, :].astype(F32), dh[r, :]
+            g, u, dhid = gb[b, r, :].astype(F32), ub[b, r, :].astype(F32), dh[r, :]
             g2 = g * g
             t = jnp.tanh(g * (0.7978845608028654 + (0.7978845608028654 * 0.044715) * g2))
             cdf = 0.5 + 0.5 * t
             act = g * cdf
             slope = cdf + (0.5 * g) * (1.0 - t * t) * (0.7978845608028654 + (3 * 0.7978845608028654 * 0.044715) * g2)
-            du[index, r, :] = (d * act).astype(BF16)
-            dg[index, r, :] = ((d * u) * slope).astype(BF16)
+            d[index, r, width:] = (dhid * act).astype(BF16)
+            d[index, r, :width] = ((dhid * u) * slope).astype(BF16)
             gb[b, r, :] = (act * u).astype(BF16)
 
         by_rows(16, 2 * rows, pointwise)
@@ -423,12 +426,11 @@
         def column(n, _):
             cols = pl.ds(pl.multiple_of(n * tile, tile), tile)
             xt = tok[b, here, cols]
-            for a, d in enumerate((dg, du)):
-                new = lax.dot_general(xt, d[index, here, :], (((0,), (0,)), ((), ())), preferred_element_type=F32)
-                for i in range(tile // 128):
-                    for j in range(ni):
-                        k = (n * (tile // 128) + i) * ni + j
-                        acc[a, k] += new[i * 128 : (i + 1) * 128, j * 128 : (j + 1) * 128]
+            new = lax.dot_general(xt, d[index, here, :], (((0,), (0,)), ((), ())), preferred_element_type=F32)
+            for i in range(tile // 128):
+                for j in range(2 * ni):
+                    k = (n * (tile // 128) + i) * ni + j % ni
+                    acc[j // ni, k] += new[i * 128 : (i + 1) * 128, j * 128 : (j + 1) * 128]
             return 0
 
         lax.fori_loop(0, depth // tile, column, 0)
@@ -442,11 +444,10 @@
 
         def keep(r):
             there = pl.ds(pl.multiple_of((1 - core) * rows + r.start, 16), 16)
-            dg_last[r, :] = dg[c * 2 + h, there, :]
-            du_last[r, :] = du[c * 2 + h, there, :]
+            d_last[r, :] = d[c * 2 + h, there, :]
 
         by_rows(16, rows, keep)
-        from_partner(X, c, h)
+        last_to_partner().wait_recv()
 
     def finish_down():
         for i in range(ni):
@@ -462,7 +463,8 @@
         lax.fori_loop(0, ni * nj, body, 0)
 
 
-    loads = [pltpu.make_async_copy(s, d, l_sem.at[i]) for i, (s, d) in enumerate(((w_down, wd), (w_gate, wg), (w_up, wu)))]
+    pairs = (w_down, wd), (w_gate, w.at[:, :width]), (w_up, w.at[:, width:])
+    loads = [pltpu.make_async_copy(s, d, l_sem.at[i]) for i, (s, d) in enumerate(pairs)]
     for load in loads:
         load.start()
 
@@ -481,6 +483,7 @@
 
     x_from = jnp.where(is_m, X_FROM["M"], X_FROM["C"])
 
+    first_sum = jnp.where(is_m, min(k for k in sum_count if k < 100), min(k for k in sum_count if k >= 100) - 100)
     last_sum = jnp.where(is_m, max(LAST["M"]), max(LAST["C"]))
 
     def step(s, _):
@@ -541,52 +544,40 @@
         n_next = select(key + 1, sum_count)
 
         def partners(k, _):
-            partner_one(select((key + 1) * 10 + k, sum_what), k)
+            partner_one(select((key + 1) * 10 + k, sum_what), (k == 0) & (s + 1 == first_sum))
             return 0
 
         lax.fori_loop(0, n_next, partners, 0)
-        for b in range(2):
-
-            @pl.when(n_next > b)
-            def _(b=b):
-                term_to_partner(0, b).wait_send()
 
         return 0
 
     lax.fori_loop(0, STEPS, step, 0)
 
-    def rest(s, _):
-        settle(s)
-        return 0
-
-    lax.fori_loop(STEPS - RING, STEPS, rest, 0)
-    for link in (P_, D_, Y_):
-
-        @pl.when(is_m | (link != D_))
-        def _(link=link):
-            for parity in range(2):
-                half_block = parts.at[link, 0, span(0)]
-                remote(out.at[link, parity], half_block, rs_send.at[link, parity], rs_recv.at[link, 0, 0], partner).wait_send()
-
-    def left(i, _):
-        to_partner(i // 32, (i // 4) % 8, i % 4).wait_send()
-        return 0
-
-    lax.fori_loop(0, 64, left, 0)
-
-
-def finish(dx, wd, acc, dg, du, full, to_x, to_gate, to_up, to_down, rows_in, done, x_sem, d_sem, g_sem):
+    def pieces_left(sem, n):
+        some = full.at[0, pl.ds(0, n // 2), pl.ds(0, rows)]
+        remote(some, some, sem, ag_recv.at[0, 0, 0], partner).wait_send()
+
+    for r, here in enumerate((is_m, is_c)):
+
+        @pl.when(here)
+        def _(r=r):
+            for link in (P_, D_, Y_):
+                n = sum(k // 100 == r for k in send_what[link])
+                if n:
+                    pieces_left(ag_send.at[link], n)
+                    for parity in range(2):
+                        half_block = parts.at[link, 0, span(0)]
+                        remote(out.at[link, parity], half_block, rs_send.at[link, parity], rs_recv.at[link, 0, 0], partner).wait_send()
+
+    for array in (DY, X):
+        pieces_left(w_send.at[array], 32 if array == DY else 30)
+    last_to_partner().wait_send()
+    term_to_partner(0).wait_send()
+
+
+def finish(dx, wd, acc, d, rows_in, to_x, to_gate, to_up, to_down, done, d_sem, g_sem):
     depth, width = to_gate.shape
-    rows, tile, ni = rows_in.shape[0], 512, width // 128
-    tp = lax.axis_index("tp")
-    core, y, z = tp % 2, tp // 8, (tp // 2) % 4
-    half, middle = z // 2, ((z + 1) % 4) // 2
-    code = jnp.where(middle == 1, last_code("M"), last_code("C"))
-    ry, rh, mm, h = code % 2, (code // 2) % 2, (code // 4) % 2, code // 8
-    yy, hh = y + ry - 2 * y * ry, half + rh - 2 * half * rh
-    chip = yy * 4 + mm + hh * (3 - 2 * mm)
-    load = pltpu.make_async_copy(full.at[X, chip * 2 + 1 - core, pl.ds(pl.multiple_of(h * rows, rows), rows)], rows_in, x_sem.at[0])
-    load.start()
+    tile, ni = 512, width // 128
     copies = []
     for i, (result, place) in enumerate(((dx, to_x), (wd, to_down))):
         n = result.shape[0] // 4
@@ -595,7 +586,6 @@
             copies.append(pltpu.make_async_copy(result.at[here], place.at[here], d_sem.at[i, k]))
     for copy in copies:
         copy.start()
-    load.wait()
 
     def store(a, n):
         here = pl.ds(pl.multiple_of(n * tile, tile), tile)
@@ -603,14 +593,14 @@
 
     def column(n, _):
         xt = rows_in[:, pl.ds(pl.multiple_of(n * tile, tile), tile)]
-        for a, d in enumerate((dg, du)):
-            new = lax.dot_general(xt, d[...], (((0,), (0,)), ((), ())), preferred_element_type=F32)
-            for i in range(tile // 128):
-                to = pl.ds(pl.multiple_of(n * tile + i * 128, 128), 128)
-                for j in range(ni):
-                    k = (n * (tile // 128) + i) * ni + j
-                    one = acc[a, k] + new[i * 128 : (i + 1) * 128, j * 128 : (j + 1) * 128]
-                    done[a, to, j * 128 : (j + 1) * 128] = one.astype(BF16)
+        new = lax.dot_general(xt, d[...], (((0,), (0,)), ((), ())), preferred_element_type=F32)
+        for i in range(tile // 128):
+            to = pl.ds(pl.multiple_of(n * tile + i * 128, 128), 128)
+            for j in range(2 * ni):
+                k = (n * (tile // 128) + i) * ni + j % ni
+                one = acc[j // ni, k] + new[i * 128 : (i + 1) * 128, j * 128 : (j + 1) * 128]
+                done[j // ni, to, j % ni * 128 : (j % ni + 1) * 128] = one.astype(BF16)
+        for a in range(2):
             store(a, n).start()
         return 0
 
@@ -635,18 +625,16 @@
                 pltpu.VMEM((block, depth), BF16),
                 pltpu.VMEM((width, depth), BF16),
                 pltpu.VMEM((2, (depth // 128) * (width // 128), 128, 128), F32),
-                pltpu.VMEM((rows, width), BF16),
-                pltpu.VMEM((rows, width), BF16),
+                pltpu.VMEM((rows, 2 * width), BF16),
+                pltpu.VMEM((rows, depth), BF16),
                 jax.ShapeDtypeStruct((2, 2 * chips, block, depth), BF16),
                 jax.ShapeDtypeStruct((4, chips, block, depth), BF16),
             ],
             in_specs=[anywhere] * 7,
             out_specs=[inside] * 5 + [anywhere] * 2,
             scratch_shapes=[
-                pltpu.VMEM((depth, width), BF16),
-                pltpu.VMEM((depth, width), BF16),
-                pltpu.VMEM((2 * chips, 2 * rows, width), BF16),
-                pltpu.VMEM((2 * chips, 2 * rows, width), BF16),
+                pltpu.VMEM((depth, 2 * width), BF16),
+                pltpu.VMEM((2 * chips, 2 * rows, 2 * width), BF16),
                 pltpu.VMEM((2, 2 * rows, depth), BF16),
                 pltpu.VMEM((2, 2 * rows, width), BF16),
                 pltpu.VMEM((2, 2 * rows, width), BF16),
@@ -654,39 +642,38 @@
                 pltpu.VMEM((rows, depth), F32),
                 pltpu.VMEM((4, rows, depth), BF16),
                 pltpu.VMEM((3, 2, rows, depth), BF16),
-                pltpu.VMEM((2, rows, depth), BF16),
+                pltpu.VMEM((rows, depth), BF16),
                 dma((2, chips, 4)),
-                dma((3, RING)),
+                dma((3,)),
                 dma((2, chips, 4)),
-                dma((2, chips, 4)),
+                dma((2,)),
                 dma((4, chips, 2)),
                 dma((3, 2)),
-                dma((2,)),
+                dma(()),
+                dma(()),
                 dma((3,)),
                 dma((2, 2)),
                 dma((2, 2)),
                 dma((2, 2)),
                 dma((4,)),
             ],
-            compiler_params=pltpu.CompilerParams(collective_id=0, has_side_effects=True, vmem_limit_bytes=47950000),
+            compiler_params=pltpu.CompilerParams(collective_id=0, has_side_effects=True, vmem_limit_bytes=46900000),
             cost_estimate=pl.CostEstimate(flops=flops, bytes_accessed=12 * tokens * depth, transcendentals=tokens * width),
             name="mlp_backward",
         )(x, dy, gate, up, w_gate, w_up, w_down)
         return pl.pallas_call(
             finish,
             out_shape=[jax.ShapeDtypeStruct(a.shape, BF16) for a in (dy, w_gate, w_up, w_down)],
-            in_specs=[inside] * 5 + [anywhere],
+            in_specs=[inside] * 5,
             out_specs=[anywhere] * 4,
             scratch_shapes=[
-                pltpu.VMEM((rows, depth), BF16),
                 pltpu.VMEM((2, depth, width), BF16),
-                dma((1,)),
                 dma((2, 4)),
                 dma((2, depth // 512)),
             ],
             compiler_params=pltpu.CompilerParams(vmem_limit_bytes=2**24),
             name="finish",
-        )(*outs[:6])
+        )(*outs[:5])
 
     rows_, cols_ = P(("dp", "tp"), None), P("dp", "tp")
     return jax.shard_map(

time: 418 us -> 409 us (0.978)
  Pallas kernels: 417 us -> 409 us
    pallas_call x1, Pallas kernels: 410 us -> 404 us  [step(): pl.pallas_call(kernel, out_shape=[pltpu.VMEM((block, depth), BF16), pltpu...]
where the time goes in v5:
time: 409 us
  Pallas kernels  409 us (100%)
    pallas_call x1, Pallas kernels, step(): pl.pallas_call(kernel, out_shape=[pltpu.VMEM((block, depth), BF16), pltpu...  404 us

profile of v5, /device:TPU:0, one launch (start us, length us, event | category | flops | bytes accessed | tf_op | source)
XLA Modules:
  0.0 409.2 jit_solution(17965967907070529724)
XLA Ops:
  0.6 403.9 %mlp_backward.1 = (bf16[416,2560]{1,0:T(8,128)(2,1)S(1)}, bf16[640,2560]{1,0:T(8,128)(2,1)S(1)}, f32[2,100,128,128]{3,2,1,0:T(8,128)S(1)}, bf16[208,1280]{1,0:T(...) custom-call(bf16[416,2560]{1,0:T(8,128)(2,1)} %x.1, ...), custom_call_target="tpu_custom_call" | custom-call | flops 130862284800 | bytes 204472320 | tf_op jit(solution)/shard_map/mlp_backward/pallas_call | solution.py:622
  404.5 4.7 %finish.1 = (bf16[416,2560]{1,0:T(8,128)(2,1)}, bf16[2560,640]{1,0:T(8,128)(2,1)}, bf16[2560,640]{1,0:T(8,128)(2,1)}, bf16[640,2560]{1,0:T(8,128)(2,1)}) custom-call(bf16[416,2560]{1,0:T(8,128)(2,1)S(1)} %get-tuple-element.9.dx, bf16[640,2560]{1,0:T(8,128)(2,1)S(1)} %get-tuple-element.10.wd, f32[2,100,128,128]{3,2,1,0:T(8,128)S(1)} %get-tuple-element.11.acc, ...), custom_call_target="tpu_custom_call" | custom-call | tf_op jit(solution)/shard_map/finish/pallas_call | solution.py:664

commit v6 on v5

--- a/solution.py
+++ b/solution.py
@@ -15,40 +15,40 @@
 
 START = {
     "a": [
-        "d00C0", "x00C0", "d01M1", "d01C0", "d00M1", "d01C1", "d01M0", "d00C1", "d00M0", "s10M1", "x00C1", "x01C1",
-        "x00M0", "x01C0", "s10M0", "x01M0", "x01M1",
+        "d00C0", "d00M0", "d00M1", "d01C1", "d01M1", "d01M0", "x00C1", "s10M2", "d01C0", "d00C1", "s10M0", "x00C0",
+        "x01C1", "x00M0", "x00M1", "x01M1", "x01C0",
     ],
     "b": [
-        "d00M1", "d01M1", "d01C0", "d00M0", "d01C1", "d01M0", "x00M1", "s10M1", "x01M1", "s10M0", "x01C1", "x00M0",
-        "x01C0", "x10M1", "x01M0", "s00C1", "s00C0",
+        "d00M0", "d00M1", "d01C1", "d01M1", "d01M0", "s10M2", "x01M1", "d01C0", "s10M0", "x00M1", "x01C0", "x01C1",
+        "x00M0", "x01M0", "x11M0", "s00C1", "s00C0",
     ],
     "c": [
-        "d00C0", "x00C1", "d00C1", "s10C0", "x00C0", "s11M1", "s11C0", "s01C1", "s11C1", "s01M0", "s10C1", "s11M0",
-        "s01C0", "s01M1", "s00M1", "x10C1", "s00M0",
+        "d00C1", "d00C0", "x00C1", "s10C0", "x00C0", "s01C1", "s11C1", "s01M0", "x10C7", "s11M0", "s01C0", "s11C0",
+        "s10C1", "s11M1", "s00M0", "s01M1", "s10M3", "s00M1",
     ],
     "d": [
-        "d00M1", "d00C0", "x10M0", "d00C1", "d00M0", "d10M1", "x00C1", "x00M1", "d10M0", "s01C1", "s11C1", "x00C0",
-        "x10M1", "x00M0", "s01C0", "s01M1", "s01M0",
+        "d00M0", "d00C1", "d00M1", "d00C0", "d10M1", "x00M1", "d10M0", "s01C1", "s11C1", "x00C0", "x00C1", "x10M1",
+        "x00M0", "x10M0", "s01C0", "s01M0", "s01M1",
     ],
     "e": [
-        "x00M0", "d00C0", "d01C0", "d00C1", "d00M1", "d01C1", "d00M0", "x01C1", "s11C0", "s11M1", "s10C0", "x00M1",
-        "x01C0", "s10C1", "s11M0", "x00C0",
+        "d00M1", "d00C1", "d01C1", "d00C0", "d01C0", "d00M0", "x00M0", "s10C0", "x00C6", "x00C0", "x00M1", "s11M0",
+        "x01C0", "s11C0", "s10C1", "s11M1", "x01C1", "s10M3",
     ],
 }
 TOKENS = {
     "M": [
-        "0d00M0", "1d00M1", "4d01M1", "4d00C0", "6d10C0", "6d01C0", "8d11C0", "8d00C1", "10d01C1", "10d10C1", "12d10M1", "12d01M0",
-        "14d11M1", "14d11C1", "16d10M0", "20d11M0", "21x00M0", "21x00M1", "22x10M0", "22x00C1", "23x11M0", "23x00C0", "24x01C1", "24x01M1",
-        "25x11C1", "26x01C0", "26x10M1", "28x11C0", "28x11M1", "30x01M0", "34x10C1", "34x10C0",
+        "0d00M0", "1d00M1", "4d10M1", "4d00C1", "5d01M0", "6d01C1", "6d10C1", "7d00C0", "8d11C1", "8d01M1", "10d10C0", "10d01C0",
+        "12d11C0", "12d11M1", "14d10M0", "16d11M0", "17x00M0", "17x00M1", "18x00C1", "18x00C0", "19x01M1", "19x10M0", "20x10C1", "21x10C0",
+        "22x01C0", "23x10M1", "24x01C1", "26x11M1", "27x11C0", "28x01M0", "30x11M0", "35x11C1",
     ],
     "C": [
-        "0d00C0", "1d00C1", "4d10C0", "4d00M1", "6d01M1", "8d11M1", "8d01C0", "10d11C0", "10d00M0", "12d01C1", "12d10M1", "14d11C1",
-        "14d01M0", "16d11M0", "18d10C1", "20d10M0", "21x00C0", "21x00C1", "22x10C0", "22x00M1", "23x01M1", "24x10C1", "24x01C1", "26x00M0",
-        "26x11C1", "28x01C0", "28x10M0", "30x10M1", "30x11C0", "32x01M0", "34x11M0", "36x11M1",
+        "0d00C0", "1d00C1", "4d10C0", "4d00M0", "6d10M0", "6d00M1", "8d01C1", "8d10M1", "10d11C1", "10d01M1", "12d01M0", "12d11M1",
+        "14d11M0", "18d01C0", "20d11C0", "22d10C1", "23x00C0", "23x00C1", "24x01M1", "24x10C1", "25x00M1", "25x01C0", "26x01C1", "26x10C0",
+        "28x00M0", "28x11C1", "30x01M0", "30x10M0", "32x10M1", "32x11M0", "34x11M1", "36x11C0",
     ],
 }
-X_FROM = {"M": 21, "C": 21}
-LAST = {"M": (35, 33), "C": (35, 33)}
+X_FROM = {"M": 17, "C": 23}
+LAST = {"M": (33, 35), "C": (35, 33)}
 STEPS = 37
 
 
@@ -72,43 +72,54 @@
 
 def plan():
     send, recv = ({P_: {}, D_: {}, Y_: {}} for _ in range(2))
-    sums, terms = {"M": {}, "C": {}}, {}
+    sums, terms, sent = {"M": {}, "C": {}}, {}, {}
     for name, entries in START.items():
         sender, receiver, link = LINKS[name]
-        t = count = 0
+        t = 0
         for what in entries:
             if what[0] == "+":
                 t += int(what)
                 continue
-            kind, unit, h = what[0], what[1:4], int(what[4])
+            kind, unit, part = what[0], what[1:4], int(what[4])
             there = seen_by_receiver(unit, link)
             if kind == "s":
-                sums[sender].setdefault(t, []).append((unit, h, link, count % 2, count >= 2, 0))
-                terms.setdefault((receiver, there, h), []).append(link)
-                count += 1
-            for k in range(0 if kind == "s" else 2):
-                code = 1 + "dx".index(kind) + 16 * (2 * h + k)
-                send[link][ROLES.index(sender) * 100 + t + k] = code + 2 * pack(unit)
-                recv[link][ROLES.index(receiver) * 100 + t + k + 2] = code + 2 * pack(there)
-            t += 2
+                h, part = (1, part - 1) if part > 1 else (part, 0)
+                before = sent.setdefault((sender, link), [])
+                sums[sender].setdefault(t, []).append((unit, h, part, link, len(before) % 2, before[-2] + 1 if len(before) > 1 else 0, 0))
+                before.append(part)
+                terms.setdefault((receiver, there, h), []).append((link, part))
+                t += 1 if part == 2 else 2
+                continue
+            for p in (2 * part, 2 * part + 1) if part < 2 else (part - 4,):
+                code = 1 + "dx".index(kind) + 16 * p
+                send[link][ROLES.index(sender) * 100 + t] = code + 2 * pack(unit)
+                recv[link][ROLES.index(receiver) * 100 + t + 2] = code + 2 * pack(there)
+                t += 1
     for role in ROLES:
         for h in range(2):
             early = h == (LAST[role][1] >= LAST[role][0])
-            sums[role].setdefault(LAST[role][h], []).insert(0, ("00" + role, h, 3, 0, 0, early))
+            sums[role].setdefault(LAST[role][h], []).insert(0, ("00" + role, h, 0, 3, 0, 0, early))
     sum_count, sum_what, tok_count, tok_what = {}, {}, {}, {}
     for r, role in enumerate(ROLES):
-        for t, entries in sums[role].items():
+        met = set()
+        for t, entries in sorted(sums[role].items()):
             sum_count[r * 100 + t] = len(entries)
-            for k, (unit, h, link, parity, before, early) in enumerate(entries):
-                code = pack(unit) + 8 * h + 16 * sum(1 << i for i in terms.get((role, unit, h), []))
-                sum_what[(r * 100 + t) * 10 + k] = code + 128 * link + 512 * parity + 1024 * before + 2048 * early
+            for k, (unit, h, part, link, parity, before, early) in enumerate(entries):
+                mine = [(i, p) for i, p in terms.get((role, unit, h), []) if part in (0, p)]
+                odd = [(i, p) for i, p in mine if p]
+                code = pack(unit) + 8 * h + 16 * sum(1 << i for i, _ in mine) + 128 * link + 512 * parity + 1024 * before
+                code += 4096 * early + 8192 * part + 2**17 * ((unit, h) in met)
+                if odd:
+                    code += 2**15 * (odd[0][1] + 0) + 2**18 * odd[0][0]
+                met.add((unit, h))
+                sum_what[(r * 100 + t) * 10 + k] = code
         for what in TOKENS[role]:
             t, kind, unit, h = int(what[:-5]), what[-5], what[-4:-1], int(what[-1])
             k = tok_count.get(r * 100 + t, 0)
             tok_count[r * 100 + t] = k + 1
             code = pack(unit) + 8 * h + 16 * "dx".index(kind)
             tok_what[(r * 100 + t) * 10 + k] = code + 32 * (what is TOKENS[role][-1])
-    return send, recv, sum_count, sum_what, tok_count, tok_what
+    return send, recv, sum_count, sum_what, tok_count, tok_what, sent
 
 
 def last_code(role):
@@ -124,11 +135,11 @@
 ):
     block, depth = dy.shape
     width = gate.shape[1]
-    rows, quarter = block // 2, block // 4
+    rows, quarter, blocks = block // 2, block // 4, full.shape[1] // 2
     tile = 512
     nj, ni = depth // 128, width // 128
     own_in = {DY: dy, X: x}
-    send_what, recv_what, sum_count, sum_what, tok_count, tok_what = plan()
+    send_what, recv_what, sum_count, sum_what, tok_count, tok_what, sent = plan()
 
     tp = lax.axis_index("tp")
     core, chip = tp % 2, tp // 2
@@ -163,12 +174,25 @@
             src_ref=src, dst_ref=dst, send_sem=send, recv_sem=recv, device_id={"tp": to}, device_id_type=MESH
         )
 
-    def by_rows(step, n_rows, fn):
+    def by_rows(step, n_rows, fn, start=0):
         def body(i, _):
             fn(pl.ds(pl.multiple_of(i * step, step), step))
             return 0
 
-        lax.fori_loop(0, n_rows // step, body, 0)
+        lax.fori_loop(start // step, n_rows // step, body, 0)
+
+    cut = rows * 3 // 4 // 16 * 16
+    part_rows = ((0, rows), (0, cut), (cut, rows - cut))
+
+    def bounds(part):
+        return jnp.where(part == 2, cut, 0), jnp.where(part == 1, cut, rows)
+
+    def in_part(part, fn):
+        for i in range(3):
+
+            @pl.when(part == i)
+            def _(i=i):
+                fn(*part_rows[i])
 
 
     def on_link(link, code, src=None):
@@ -253,27 +277,53 @@
 
     def reduce_one(code):
         c, h = chip_packed(code), (code // 8) % 2
-        mask, link, parity, before = (code // 16) % 8, (code // 128) % 4, (code // 512) % 2, (code // 1024) % 2
+        mask, link, parity, before = (code // 16) % 8, (code // 128) % 4, (code // 512) % 2, (code // 1024) % 4
+        early, part, again = (code // 4096) % 2 == 1, (code // 8192) % 4, (code // 2**17) % 2 == 1
+        odd_part, odd = (code // 2**15) % 4, code // 2**18
         bits = {P_: mask % 2 == 1, D_: (mask // 2) % 2 == 1, Y_: mask // 4 == 1}
-
-        def term_in(kind):
-            return pltpu.make_async_copy(parts.at[kind, c, span(h)], ext.at[kind], e_sem.at[kind])
+        part_of = {P_: jnp.where(odd == P_, odd_part, 0), D_: jnp.int32(0), Y_: jnp.where(odd == Y_, odd_part, 0), W_: jnp.int32(0)}
+
+        def there(lo, n):
+            return pl.ds(pl.multiple_of(h * rows + lo, 16), n)
+
+        def term_in(kind, lo, n):
+            return pltpu.make_async_copy(parts.at[kind, c, there(lo, n)], ext.at[kind, pl.ds(lo, n)], e_sem.at[kind])
+
+        def with_term(kind, fn):
+            if kind in (P_, Y_):
+                in_part(part_of[kind], fn)
+            else:
+                fn(0, rows)
+
+        def arrived(kind):
+            def wait(lo, n):
+                here = ext.at[kind, pl.ds(lo, n)]
+                remote(here, parts.at[kind, c, there(lo, n)], p_send, rs_recv.at[kind, c, h], partner).wait_recv()
+
+            with_term(kind, wait)
 
         def fetch(kind):
-            remote(ext.at[kind], parts.at[kind, c, span(h)], p_send, rs_recv.at[kind, c, h], partner).wait_recv()
-            term_in(kind).start()
-
-        def send_term(to):
-            return remote(out.at[link, parity], parts.at[link, c, span(h)], rs_send.at[link, parity], rs_recv.at[link, c, h], to)
+            with_term(kind, lambda lo, n: term_in(kind, lo, n).start())
+
+        def send_term(to, lo, n):
+            return remote(
+                out.at[link, parity, pl.ds(lo, n)], parts.at[link, c, there(lo, n)], rs_send.at[link, parity],
+                rs_recv.at[link, c, h], to,
+            )
+
+        @pl.when(jnp.logical_not(again))
+        def _():
+            arrived(W_)
 
         fetch(W_)
         for kind in (P_, D_, Y_):
 
             @pl.when(bits[kind] & (link != 3))
             def _(kind=kind):
+                arrived(kind)
                 fetch(kind)
 
-        @pl.when(code < 2048)
+        @pl.when(jnp.logical_not(early))
         def _():
             dx_term(code, core)
 
@@ -281,20 +331,22 @@
 
             @pl.when(bits[kind] & (link == 3))
             def _(kind=kind):
+                arrived(kind)
                 fetch(kind)
 
         for kind in (P_, D_, Y_):
 
             @pl.when(bits[kind])
             def _(kind=kind):
-                term_in(kind).wait()
+                with_term(kind, lambda lo, n: term_in(kind, lo, n).wait())
 
                 def add(r):
                     total[r, :] += ext[kind, r, :].astype(F32)
 
-                by_rows(16, rows, add)
-
-        term_in(W_).wait()
+                lo, hi = bounds(part_of[kind])
+                by_rows(16, hi, add, lo)
+
+        term_in(W_, 0, rows).wait()
 
         @pl.when(link == 3)
         def _():
@@ -307,16 +359,14 @@
         @pl.when(link != 3)
         def _():
             to = jnp.where(link == P_, at_link[P_], jnp.where(link == D_, at_link[D_], at_link[Y_]))
-
-            @pl.when(before == 1)
-            def _():
-                send_term(to).wait_send()
+            in_part(before - 1, lambda lo, n: send_term(to, lo, n).wait_send())
 
             def round_(r):
                 out[link, parity, r, :] = (total[r, :] + ext[W_, r, :].astype(F32)).astype(BF16)
 
-            by_rows(16, rows, round_)
-            send_term(to).start()
+            lo, hi = bounds(part)
+            by_rows(16, hi, round_, lo)
+            in_part(part, lambda lo, n: send_term(to, lo, n).start())
 
     def term_to_partner(code):
         c, h = chip_packed(code), (code // 8) % 2
@@ -538,13 +588,25 @@
 
             return 0
 
-        lax.fori_loop(0, select(key, sum_count), sums, 0)
-        lax.fori_loop(0, n_tok, tokens, 0)
+        n_sum, tokens_first = select(key, sum_count), is_m & (s == last_sum)
+
+        def phase(p, _):
+            now = (p == 0) != tokens_first
+            lax.fori_loop(0, jnp.where(now, n_sum, 0), sums, 0)
+            lax.fori_loop(0, jnp.where(now, 0, n_tok), tokens, 0)
+            return 0
+
+        lax.fori_loop(0, 2, phase, 0)
 
         n_next = select(key + 1, sum_count)
 
         def partners(k, _):
-            partner_one(select((key + 1) * 10 + k, sum_what), (k == 0) & (s + 1 == first_sum))
+            code = select((key + 1) * 10 + k, sum_what)
+
+            @pl.when((code // 2**17) % 2 == 0)
+            def _():
+                partner_one(code, (k == 0) & (s + 1 == first_sum))
+
             return 0
 
         lax.fori_loop(0, n_next, partners, 0)
@@ -554,7 +616,9 @@
     lax.fori_loop(0, STEPS, step, 0)
 
     def pieces_left(sem, n):
-        some = full.at[0, pl.ds(0, n // 2), pl.ds(0, rows)]
+        sizes = [(b, n * quarter // b) for b in range(1, 2 * blocks) if n * quarter % b == 0 and n * quarter // b <= block]
+        b, m = min(sizes, key=lambda size: size[1] % 8 > 0)
+        some = full.at[0, pl.ds(0, b), pl.ds(0, m)]
         remote(some, some, sem, ag_recv.at[0, 0, 0], partner).wait_send()
 
     for r, here in enumerate((is_m, is_c)):
@@ -565,9 +629,11 @@
                 n = sum(k // 100 == r for k in send_what[link])
                 if n:
                     pieces_left(ag_send.at[link], n)
-                    for parity in range(2):
-                        half_block = parts.at[link, 0, span(0)]
-                        remote(out.at[link, parity], half_block, rs_send.at[link, parity], rs_recv.at[link, 0, 0], partner).wait_send()
+                    parts_sent = sent[ROLES[r], link]
+                    for i in (len(parts_sent) - 2, len(parts_sent) - 1):
+                        lo, m = part_rows[parts_sent[i]]
+                        here, there = out.at[link, i % 2, pl.ds(lo, m)], parts.at[link, 0, pl.ds(lo, m)]
+                        remote(here, there, rs_send.at[link, i % 2], rs_recv.at[link, 0, 0], partner).wait_send()
 
     for array in (DY, X):
         pieces_left(w_send.at[array], 32 if array == DY else 30)

time: 409 us -> 409 us (level)
  no operation moved by 1% of the time
where the time goes in v6:
time: 409 us; the launch traced here: 408 us
  Pallas kernels  408 us (100%)
    pallas_call x1, Pallas kernels, step(): pl.pallas_call(kernel, out_shape=[pltpu.VMEM((block, depth), BF16), pltpu...  403 us

profile of v6, /device:TPU:0, one launch (start us, length us, event | category | flops | bytes accessed | tf_op | source)
XLA Modules:
  0.0 408.2 jit_solution(12119601288061463841)
XLA Ops:
  0.6 402.9 %mlp_backward.1 = (bf16[416,2560]{1,0:T(8,128)(2,1)S(1)}, bf16[640,2560]{1,0:T(8,128)(2,1)S(1)}, f32[2,100,128,128]{3,2,1,0:T(8,128)S(1)}, bf16[208,1280]{1,0:T(...) custom-call(bf16[416,2560]{1,0:T(8,128)(2,1)} %x.1, ...), custom_call_target="tpu_custom_call" | custom-call | flops 130862284800 | bytes 204472320 | tf_op jit(solution)/shard_map/mlp_backward/pallas_call | solution.py:688
  403.6 4.7 %finish.1 = (bf16[416,2560]{1,0:T(8,128)(2,1)}, bf16[2560,640]{1,0:T(8,128)(2,1)}, bf16[2560,640]{1,0:T(8,128)(2,1)}, bf16[640,2560]{1,0:T(8,128)(2,1)}) custom-call(bf16[416,2560]{1,0:T(8,128)(2,1)S(1)} %get-tuple-element.9.dx, bf16[640,2560]{1,0:T(8,128)(2,1)S(1)} %get-tuple-element.10.wd, f32[2,100,128,128]{3,2,1,0:T(8,128)S(1)} %get-tuple-element.11.acc, ...), custom_call_target="tpu_custom_call" | custom-call | tf_op jit(solution)/shard_map/finish/pallas_call | solution.py:730

commit v7 on v6

--- a/solution.py
+++ b/solution.py
@@ -8,6 +8,9 @@
 MESH = pl.DeviceIdType.MESH
 F32, BF16 = jnp.float32, jnp.bfloat16
 
+LANES = 128
+ROOT = 0.7978845608028654
+BY_ROWS, BY_COLUMNS = (((0,), (0,)), ((), ())), (((1,), (1,)), ((), ()))
 P_, D_, Y_, W_ = 0, 1, 2, 3
 DY, X = 0, 1
 ROLES = "MC"
@@ -15,40 +18,40 @@
 
 START = {
     "a": [
-        "d00C0", "d00M0", "d00M1", "d01C1", "d01M1", "d01M0", "x00C1", "s10M2", "d01C0", "d00C1", "s10M0", "x00C0",
-        "x01C1", "x00M0", "x00M1", "x01M1", "x01C0",
+        "d00C1", "d00M0", "d00C0", "d01C0", "d01M1", "d00M1", "d01C1", "s10M0", "d01M0", "s10M2", "x00M1", "x00C0",
+        "x00C1", "x01C0", "x01M0", "x01M1", "x00M0",
     ],
     "b": [
-        "d00M0", "d00M1", "d01C1", "d01M1", "d01M0", "s10M2", "x01M1", "d01C0", "s10M0", "x00M1", "x01C0", "x01C1",
-        "x00M0", "x01M0", "x11M0", "s00C1", "s00C0",
+        "d00M0", "d00M1", "d01C0", "d01M1", "s10M0", "d01C1", "s10M2", "d01M0", "x01M0", "x00M1", "x00M0", "x01C1",
+        "x01C0", "x11C1", "x01M1", "s00C0", "s00C1",
     ],
     "c": [
-        "d00C1", "d00C0", "x00C1", "s10C0", "x00C0", "s01C1", "s11C1", "s01M0", "x10C7", "s11M0", "s01C0", "s11C0",
-        "s10C1", "s11M1", "s00M0", "s01M1", "s10M3", "s00M1",
+        "d00C0", "x00C0", "d00C1", "s10C1", "x00C1", "s01C0", "s11C0", "s10C0", "s01C1", "s11C1", "s01M1", "s10M3",
+        "s11M1", "s11M0", "x10C7", "s01M0", "s00M0", "s00M1",
     ],
     "d": [
-        "d00M0", "d00C1", "d00M1", "d00C0", "d10M1", "x00M1", "d10M0", "s01C1", "s11C1", "x00C0", "x00C1", "x10M1",
-        "x00M0", "x10M0", "s01C0", "s01M0", "s01M1",
+        "d00M1", "d00C0", "d10M0", "d00C1", "d10M1", "x00M0", "d00M0", "s01C0", "x00C0", "x00C1", "x10M0", "s11C0",
+        "s01C1", "x00M1", "x10M1", "s01M1", "s01M0",
     ],
     "e": [
-        "d00M1", "d00C1", "d01C1", "d00C0", "d01C0", "d00M0", "x00M0", "s10C0", "x00C6", "x00C0", "x00M1", "s11M0",
-        "x01C0", "s11C0", "s10C1", "s11M1", "x01C1", "s10M3",
+        "x00M1", "d00M0", "d00C0", "d00M1", "d00C1", "d01C0", "d01C1", "s10C1", "x00C6", "x00M0", "x01C0", "s11C1",
+        "x01C1", "s10C0", "s11M1", "s11M0", "x00C0", "s10M3",
     ],
 }
 TOKENS = {
     "M": [
-        "0d00M0", "1d00M1", "4d10M1", "4d00C1", "5d01M0", "6d01C1", "6d10C1", "7d00C0", "8d11C1", "8d01M1", "10d10C0", "10d01C0",
-        "12d11C0", "12d11M1", "14d10M0", "16d11M0", "17x00M0", "17x00M1", "18x00C1", "18x00C0", "19x01M1", "19x10M0", "20x10C1", "21x10C0",
-        "22x01C0", "23x10M1", "24x01C1", "26x11M1", "27x11C0", "28x01M0", "30x11M0", "35x11C1",
+        "0d00M0", "1d00M1", "4d00C0", "4d01M1", "6d10M0", "6d01C0", "8d10C0", "8d11M0", "9d00C1", "10d10M1", "10d01C1", "12d10C1",
+        "12d11M1", "14d11C0", "16d11C1", "16d01M0", "17x00M0", "17x00M1", "18x10M1", "18x00C0", "19x00C1", "19x01M0", "20x01C0", "21x10M0",
+        "22x01C1", "23x11C0", "24x11M0", "27x11C1", "30x01M1", "30x10C1", "32x11M1", "35x10C0",
     ],
     "C": [
-        "0d00C0", "1d00C1", "4d10C0", "4d00M0", "6d10M0", "6d00M1", "8d01C1", "8d10M1", "10d11C1", "10d01M1", "12d01M0", "12d11M1",
-        "14d11M0", "18d01C0", "20d11C0", "22d10C1", "23x00C0", "23x00C1", "24x01M1", "24x10C1", "25x00M1", "25x01C0", "26x01C1", "26x10C0",
-        "28x00M0", "28x11C1", "30x01M0", "30x10M0", "32x10M1", "32x11M0", "34x11M1", "36x11C0",
+        "0d00C0", "1d00C1", "4d10C1", "4d00M0", "6d10M0", "6d00M1", "8d01C0", "8d10C0", "10d11C0", "10d01M1", "12d11M1", "14d01C1",
+        "14d10M1", "16d11C1", "18d01M0", "20d11M0", "21x00C0", "21x00C1", "22x01M0", "22x00M1", "24x00M0", "24x10M1", "26x01C1", "26x10C0",
+        "28x01C0", "28x10C1", "30x11C0", "30x11C1", "32x01M1", "32x11M0", "34x11M1", "36x10M0",
     ],
 }
-X_FROM = {"M": 17, "C": 23}
-LAST = {"M": (33, 35), "C": (35, 33)}
+X_FROM = {"M": 17, "C": 21}
+LAST = {"M": (35, 35), "C": (33, 35)}
 STEPS = 37
 
 
@@ -61,6 +64,14 @@
 
 def pack(unit):
     return int(unit[0]) + 2 * int(unit[1]) + 4 * (unit[2] == "M")
+
+
+def lanes(i):
+    return slice(i * LANES, (i + 1) * LANES)
+
+
+def half_in(code):
+    return (code // 8) % 2
 
 
 def select(key, table):
@@ -137,7 +148,7 @@
     width = gate.shape[1]
     rows, quarter, blocks = block // 2, block // 4, full.shape[1] // 2
     tile = 512
-    nj, ni = depth // 128, width // 128
+    nj, ni = depth // LANES, width // LANES
     own_in = {DY: dy, X: x}
     send_what, recv_what, sum_count, sum_what, tok_count, tok_what, sent = plan()
 
@@ -263,20 +274,20 @@
 
 
     def dx_term(code, plane):
-        index = chip_packed(code) * 2 + (code // 8) % 2
+        index = chip_packed(code) * 2 + half_in(code)
         here = span(plane)
 
         def column(n, _):
             cols = pl.ds(pl.multiple_of(n * tile, tile), tile)
             total[:, cols] = lax.dot_general(
-                d[index, here, :], w[cols, :], (((1,), (1,)), ((), ())), preferred_element_type=F32
+                d[index, here, :], w[cols, :], BY_COLUMNS, preferred_element_type=F32
             )
             return 0
 
         lax.fori_loop(0, depth // tile, column, 0)
 
     def reduce_one(code):
-        c, h = chip_packed(code), (code // 8) % 2
+        c, h = chip_packed(code), half_in(code)
         mask, link, parity, before = (code // 16) % 8, (code // 128) % 4, (code // 512) % 2, (code // 1024) % 4
         early, part, again = (code // 4096) % 2 == 1, (code // 8192) % 4, (code // 2**17) % 2 == 1
         odd_part, odd = (code // 2**15) % 4, code // 2**18
@@ -369,7 +380,7 @@
             in_part(part, lambda lo, n: send_term(to, lo, n).start())
 
     def term_to_partner(code):
-        c, h = chip_packed(code), (code // 8) % 2
+        c, h = chip_packed(code), half_in(code)
         return remote(outw, parts.at[W_, c, span(h)], p_send, rs_recv.at[W_, c, h], partner)
 
     def partner_one(code, first):
@@ -386,23 +397,13 @@
         term_to_partner(code).start()
 
 
-    def last_in(code, b):
-        c, h = chip_packed(code), (code // 8) % 2
-        src = full.at[X, c * 2 + core, span(h)]
-        return pltpu.make_async_copy(src, tok.at[b, span(core)], tok_sem.at[b, core])
-
     def tok_in(code, b, start):
         @pl.when(code < 32)
         def _():
             pair_in(code, b, start)
 
-        @pl.when(code >= 32)
-        def _():
-            copy = last_in(code, b)
-            copy.start() if start else copy.wait()
-
     def pair_in(code, b, start):
-        c, h, array = chip_packed(code), (code // 8) % 2, (code // 16) % 2
+        c, h, array = chip_packed(code), half_in(code), (code // 16) % 2
         mine = c == chip
         for plane in range(2):
             blk = c * 2 + plane
@@ -445,16 +446,16 @@
                     pltpu.make_async_copy(own_in[a].at[span(h)], dst, sem).start()
 
     def work_dy(code, b):
-        index = chip_packed(code) * 2 + (code // 8) % 2
-        dh[...] = lax.dot_general(tok[b], wd[...], (((1,), (1,)), ((), ())), preferred_element_type=F32)
+        index = chip_packed(code) * 2 + half_in(code)
+        dh[...] = lax.dot_general(tok[b], wd[...], BY_COLUMNS, preferred_element_type=F32)
 
         def pointwise(r):
             g, u, dhid = gb[b, r, :].astype(F32), ub[b, r, :].astype(F32), dh[r, :]
             g2 = g * g
-            t = jnp.tanh(g * (0.7978845608028654 + (0.7978845608028654 * 0.044715) * g2))
+            t = jnp.tanh(g * (ROOT + (ROOT * 0.044715) * g2))
             cdf = 0.5 + 0.5 * t
             act = g * cdf
-            slope = cdf + (0.5 * g) * (1.0 - t * t) * (0.7978845608028654 + (3 * 0.7978845608028654 * 0.044715) * g2)
+            slope = cdf + (0.5 * g) * (1.0 - t * t) * (ROOT + (3 * ROOT * 0.044715) * g2)
             d[index, r, width:] = (dhid * act).astype(BF16)
             d[index, r, :width] = ((dhid * u) * slope).astype(BF16)
             gb[b, r, :] = (act * u).astype(BF16)
@@ -463,51 +464,51 @@
 
         def column(n, _):
             cols = pl.ds(pl.multiple_of(n * tile, tile), tile)
-            new = lax.dot_general(gb[b], tok[b, :, cols], (((0,), (0,)), ((), ())), preferred_element_type=F32)
+            new = lax.dot_general(gb[b], tok[b, :, cols], BY_ROWS, preferred_element_type=F32)
             for i in range(ni):
-                for j in range(tile // 128):
-                    k = i * nj + n * (tile // 128) + j
-                    acc[0, k] += new[i * 128 : (i + 1) * 128, j * 128 : (j + 1) * 128]
+                for j in range(tile // LANES):
+                    k = i * nj + n * (tile // LANES) + j
+                    acc[0, k] += new[lanes(i), lanes(j)]
             return 0
 
         lax.fori_loop(0, depth // tile, column, 0)
 
-    def x_columns(index, b, here):
+    def work_x(code, b):
+        index = chip_packed(code) * 2 + half_in(code)
+
         def column(n, _):
             cols = pl.ds(pl.multiple_of(n * tile, tile), tile)
-            xt = tok[b, here, cols]
-            new = lax.dot_general(xt, d[index, here, :], (((0,), (0,)), ((), ())), preferred_element_type=F32)
-            for i in range(tile // 128):
+            new = lax.dot_general(tok[b, :, cols], d[index], BY_ROWS, preferred_element_type=F32)
+            for i in range(tile // LANES):
                 for j in range(2 * ni):
-                    k = (n * (tile // 128) + i) * ni + j % ni
-                    acc[j // ni, k] += new[i * 128 : (i + 1) * 128, j * 128 : (j + 1) * 128]
+                    k = (n * (tile // LANES) + i) * ni + j % ni
+                    acc[j // ni, k] += new[lanes(i), lanes(j)]
             return 0
 
         lax.fori_loop(0, depth // tile, column, 0)
 
-    def work_x(code, b):
-        x_columns(chip_packed(code) * 2 + (code // 8) % 2, b, slice(None))
-
-    def last_x(code, b):
-        c, h = chip_packed(code), (code // 8) % 2
-        x_columns(c * 2 + h, b, span(core))
+    def last_x(code):
+        c, h = chip_packed(code), half_in(code)
+        own = pltpu.make_async_copy(d.at[c * 2 + h, span(core)], parts.at[4, 0, 0:rows, 0 : 2 * width], tok_sem.at[0, 0])
+        own.start()
 
         def keep(r):
             there = pl.ds(pl.multiple_of((1 - core) * rows + r.start, 16), 16)
             d_last[r, :] = d[c * 2 + h, there, :]
 
         by_rows(16, rows, keep)
+        own.wait()
         last_to_partner().wait_recv()
 
     def finish_down():
         for i in range(ni):
             for j in range(nj):
-                wd[i * 128 : (i + 1) * 128, j * 128 : (j + 1) * 128] = acc[0, i * nj + j].astype(BF16)
-                acc[0, i * nj + j] = jnp.zeros((128, 128), F32)
+                wd[lanes(i), lanes(j)] = acc[0, i * nj + j].astype(BF16)
+                acc[0, i * nj + j] = jnp.zeros((LANES, LANES), F32)
 
     def clear(i):
         def body(k, _):
-            acc[i, k] = jnp.zeros((128, 128), F32)
+            acc[i, k] = jnp.zeros((LANES, LANES), F32)
             return 0
 
         lax.fori_loop(0, ni * nj, body, 0)
@@ -584,7 +585,7 @@
 
             @pl.when(code >= 32)
             def _():
-                last_x(code, b)
+                last_x(code)
 
             return 0
 
@@ -641,9 +642,24 @@
     term_to_partner(0).wait_send()
 
 
-def finish(dx, wd, acc, d, rows_in, to_x, to_gate, to_up, to_down, done, d_sem, g_sem):
+def finish(
+    dx, wd, acc, d, rows_in, full, parts, to_x, to_gate, to_up, to_down, done, d_in, rows_own, o_sem, d_sem, g_sem
+):
     depth, width = to_gate.shape
-    tile, ni = 512, width // 128
+    rows, tile, ni = rows_in.shape[0], 512, width // LANES
+    tp = lax.axis_index("tp")
+    core, y, z = tp % 2, tp // 8, (tp // 2) % 4
+    half, middle = z // 2, ((z + 1) % 4) // 2
+    code = jnp.where(middle == 1, last_code("M"), last_code("C"))
+    ry, rh, mm, h = code % 2, (code // 2) % 2, (code // 4) % 2, code // 8
+    yy, hh = y + ry - 2 * y * ry, half + rh - 2 * half * rh
+    block = (yy * 4 + mm + hh * (3 - 2 * mm)) * 2 + core
+    loads = (
+        pltpu.make_async_copy(full.at[X, block, pl.ds(pl.multiple_of(h * rows, rows), rows)], rows_own, o_sem.at[0]),
+        pltpu.make_async_copy(parts.at[4, 0, 0:rows, 0 : 2 * width], d_in, o_sem.at[1]),
+    )
+    for load in loads:
+        load.start()
     copies = []
     for i, (result, place) in enumerate(((dx, to_x), (wd, to_down))):
         n = result.shape[0] // 4
@@ -657,15 +673,19 @@
         here = pl.ds(pl.multiple_of(n * tile, tile), tile)
         return pltpu.make_async_copy(done.at[a, here], (to_gate, to_up)[a].at[here], g_sem.at[a, n])
 
+    for load in loads:
+        load.wait()
+
     def column(n, _):
-        xt = rows_in[:, pl.ds(pl.multiple_of(n * tile, tile), tile)]
-        new = lax.dot_general(xt, d[...], (((0,), (0,)), ((), ())), preferred_element_type=F32)
-        for i in range(tile // 128):
-            to = pl.ds(pl.multiple_of(n * tile + i * 128, 128), 128)
+        cols = pl.ds(pl.multiple_of(n * tile, tile), tile)
+        new = lax.dot_general(rows_in[:, cols], d[...], BY_ROWS, preferred_element_type=F32)
+        new += lax.dot_general(rows_own[:, cols], d_in[...], BY_ROWS, preferred_element_type=F32)
+        for i in range(tile // LANES):
+            to = pl.ds(pl.multiple_of(n * tile + i * LANES, LANES), LANES)
             for j in range(2 * ni):
-                k = (n * (tile // 128) + i) * ni + j % ni
-                one = acc[j // ni, k] + new[i * 128 : (i + 1) * 128, j * 128 : (j + 1) * 128]
-                done[j // ni, to, j % ni * 128 : (j % ni + 1) * 128] = one.astype(BF16)
+                a, k = j // ni, (n * (tile // LANES) + i) * ni + j % ni
+                one = acc[a, k] + new[lanes(i), lanes(j)]
+                done[a, to, j % ni * LANES : (j % ni + 1) * LANES] = one.astype(BF16)
         for a in range(2):
             store(a, n).start()
         return 0
@@ -690,11 +710,11 @@
             out_shape=[
                 pltpu.VMEM((block, depth), BF16),
                 pltpu.VMEM((width, depth), BF16),
-                pltpu.VMEM((2, (depth // 128) * (width // 128), 128, 128), F32),
+                pltpu.VMEM((2, (depth // LANES) * (width // LANES), LANES, LANES), F32),
                 pltpu.VMEM((rows, 2 * width), BF16),
                 pltpu.VMEM((rows, depth), BF16),
                 jax.ShapeDtypeStruct((2, 2 * chips, block, depth), BF16),
-                jax.ShapeDtypeStruct((4, chips, block, depth), BF16),
+                jax.ShapeDtypeStruct((5, chips, block, depth), BF16),
             ],
             in_specs=[anywhere] * 7,
             out_specs=[inside] * 5 + [anywhere] * 2,
@@ -730,16 +750,19 @@
         return pl.pallas_call(
             finish,
             out_shape=[jax.ShapeDtypeStruct(a.shape, BF16) for a in (dy, w_gate, w_up, w_down)],
-            in_specs=[inside] * 5,
+            in_specs=[inside] * 5 + [anywhere] * 2,
             out_specs=[anywhere] * 4,
             scratch_shapes=[
                 pltpu.VMEM((2, depth, width), BF16),
+                pltpu.VMEM((rows, 2 * width), BF16),
+                pltpu.VMEM((rows, depth), BF16),
+                dma((2,)),
                 dma((2, 4)),
                 dma((2, depth // 512)),
             ],
             compiler_params=pltpu.CompilerParams(vmem_limit_bytes=2**24),
             name="finish",
-        )(*outs[:5])
+        )(*outs)
 
     rows_, cols_ = P(("dp", "tp"), None), P("dp", "tp")
     return jax.shard_map(

time: 409 us -> 411 us (level); the launches traced: 408 us -> 404 us
    pallas_call x1, Pallas kernels: 403 us -> 395 us  [step(): pl.pallas_call(kernel, out_shape=[pltpu.VMEM((block, depth), BF16), pltpu...]
    pallas_call x1, Pallas kernels: 4.66 us -> 9.15 us  [step(): pl.pallas_call(finish, out_shape=[jax.ShapeDtypeStruct(a.shape, BF16) for...]
where the time goes in v7:
time: 411 us; the launch traced here: 404 us
  Pallas kernels  404 us (98%)
    pallas_call x1, Pallas kernels, step(): pl.pallas_call(kernel, out_shape=[pltpu.VMEM((block, depth), BF16), pltpu...  395 us
    pallas_call x1, Pallas kernels, step(): pl.pallas_call(finish, out_shape=[jax.ShapeDtypeStruct(a.shape, BF16) for...  9.15 us

profile of v7, /device:TPU:0, one launch (start us, length us, event | category | flops | bytes accessed | tf_op | source)
XLA Modules:
  0.0 404.3 jit_solution(6531896427970146753)
XLA Ops:
  0.6 394.6 %mlp_backward.1 = (bf16[416,2560]{1,0:T(8,128)(2,1)S(1)}, bf16[640,2560]{1,0:T(8,128)(2,1)S(1)}, f32[2,100,128,128]{3,2,1,0:T(8,128)S(1)}, bf16[208,1280]{1,0:T(...) custom-call(bf16[416,2560]{1,0:T(8,128)(2,1)} %x.1, ...), custom_call_target="tpu_custom_call" | custom-call | flops 130862284800 | bytes 204472320 | tf_op jit(solution)/shard_map/mlp_backward/pallas_call | solution.py:708
  395.2 9.1 %finish.1 = (bf16[416,2560]{1,0:T(8,128)(2,1)}, bf16[2560,640]{1,0:T(8,128)(2,1)}, bf16[2560,640]{1,0:T(8,128)(2,1)}, bf16[640,2560]{1,0:T(8,128)(2,1)}) custom-call(bf16[416,2560]{1,0:T(8,128)(2,1)S(1)} %get-tuple-element.11.dx, bf16[640,2560]{1,0:T(8,128)(2,1)S(1)} %get-tuple-element.12.wd, f32[2,100,128,128]{3,2,1,0:T(8,128)S(1)} %get-tuple-element.13.acc, ...), custom_call_target="tpu_custom_call" | custom-call | tf_op jit(solution)/shard_map/finish/pallas_call | solution.py:750

commit v8 on v7

--- a/solution.py
+++ b/solution.py
@@ -18,40 +18,40 @@
 
 START = {
     "a": [
-        "d00C1", "d00M0", "d00C0", "d01C0", "d01M1", "d00M1", "d01C1", "s10M0", "d01M0", "s10M2", "x00M1", "x00C0",
-        "x00C1", "x01C0", "x01M0", "x01M1", "x00M0",
+        "d00C0", "d00M0", "d00M1", "d01C0", "d00C1", "s10M0", "d01M1", "d01C1", "d01M0", "x01M1", "x01C1", "x00M1",
+        "x00C1", "x00M0", "s10M2", "x01C0", "x00C0",
     ],
     "b": [
-        "d00M0", "d00M1", "d01C0", "d01M1", "s10M0", "d01C1", "s10M2", "d01M0", "x01M0", "x00M1", "x00M0", "x01C1",
-        "x01C0", "x11C1", "x01M1", "s00C0", "s00C1",
+        "d00M0", "d00M1", "d01C0", "s10M0", "d01M1", "s10M2", "d01C1", "d01M0", "x01M1", "x01C1", "x00M1", "x11M0",
+        "x00M0", "x01M0", "x01C0", "s00C0", "s00C1",
     ],
     "c": [
-        "d00C0", "x00C0", "d00C1", "s10C1", "x00C1", "s01C0", "s11C0", "s10C0", "s01C1", "s11C1", "s01M1", "s10M3",
-        "s11M1", "s11M0", "x10C7", "s01M0", "s00M0", "s00M1",
+        "d00C0", "x00C0", "d00C1", "x00C1", "s10C0", "s01C0", "s11C0", "s00M0", "s10C1", "s11M1", "s11C1", "s11M0",
+        "s01C1", "s01M0", "x10C7", "s01M1", "s10M3", "s00M1",
     ],
     "d": [
-        "d00M1", "d00C0", "d10M0", "d00C1", "d10M1", "x00M0", "d00M0", "s01C0", "x00C0", "x00C1", "x10M0", "s11C0",
-        "s01C1", "x00M1", "x10M1", "s01M1", "s01M0",
+        "d00M0", "d00C0", "d00M1", "d10M0", "d10M1", "d00C1", "x10M1", "x00M1", "x00C1", "x00M0", "x10M0", "s01C0",
+        "s11C1", "x00C0", "s01C1", "s01M0", "s01M1",
     ],
     "e": [
-        "x00M1", "d00M0", "d00C0", "d00M1", "d00C1", "d01C0", "d01C1", "s10C1", "x00C6", "x00M0", "x01C0", "s11C1",
-        "x01C1", "s10C0", "s11M1", "s11M0", "x00C0", "s10M3",
+        "d00M0", "d00M1", "d01C0", "d00C1", "d00C0", "x00M1", "d01C1", "s10C0", "s11C0", "x00M0", "x01C1", "s11M1",
+        "x00C6", "s11M0", "s10C1", "x01C0", "x00C0", "s10M3",
     ],
 }
 TOKENS = {
     "M": [
-        "0d00M0", "1d00M1", "4d00C0", "4d01M1", "6d10M0", "6d01C0", "8d10C0", "8d11M0", "9d00C1", "10d10M1", "10d01C1", "12d10C1",
-        "12d11M1", "14d11C0", "16d11C1", "16d01M0", "17x00M0", "17x00M1", "18x10M1", "18x00C0", "19x00C1", "19x01M0", "20x01C0", "21x10M0",
-        "22x01C1", "23x11C0", "24x11M0", "27x11C1", "30x01M1", "30x10C1", "32x11M1", "35x10C0",
+        "0d00M0", "1d00M1", "4d10M0", "4d00C0", "5d01M0", "6d10M1", "6d01C0", "8d11C0", "8d00C1", "9d01M1", "10d11M0", "10d10C1",
+        "12d10C0", "12d11M1", "14d01C1", "16d11C1", "17x00M0", "17x00M1", "18x00C0", "18x00C1", "19x10M1", "19x11M1", "20x01M1", "20x01C1",
+        "22x01M0", "22x10M0", "24x11C1", "24x11M0", "30x01C0", "31x10C1", "33x11C0", "35x10C0",
     ],
     "C": [
-        "0d00C0", "1d00C1", "4d10C1", "4d00M0", "6d10M0", "6d00M1", "8d01C0", "8d10C0", "10d11C0", "10d01M1", "12d11M1", "14d01C1",
-        "14d10M1", "16d11C1", "18d01M0", "20d11M0", "21x00C0", "21x00C1", "22x01M0", "22x00M1", "24x00M0", "24x10M1", "26x01C1", "26x10C0",
-        "28x01C0", "28x10C1", "30x11C0", "30x11C1", "32x01M1", "32x11M0", "34x11M1", "36x10M0",
+        "0d00C0", "1d00C1", "4d10C0", "4d00M0", "6d10M0", "6d00M1", "8d01C0", "8d10M1", "10d11C0", "12d10C1", "12d01M1", "16d11M1",
+        "16d01C1", "18d11C1", "18d01M0", "20d11M0", "21x00C0", "21x00C1", "22x01M1", "22x01C1", "23x11M1", "24x00M1", "24x11C1", "26x10M1",
+        "26x11M0", "28x00M0", "28x10C1", "30x01M0", "30x10M0", "32x01C0", "34x11C0", "36x10C0",
     ],
 }
 X_FROM = {"M": 17, "C": 21}
-LAST = {"M": (35, 35), "C": (33, 35)}
+LAST = {"M": (33, 35), "C": (33, 35)}
 STEPS = 37
 
 
@@ -397,10 +397,20 @@
         term_to_partner(code).start()
 
 
+    def last_in(code, b):
+        c, h = chip_packed(code), half_in(code)
+        src = full.at[X, c * 2 + core, span(h)]
+        return pltpu.make_async_copy(src, tok.at[b, span(core)], tok_sem.at[b, core])
+
     def tok_in(code, b, start):
         @pl.when(code < 32)
         def _():
             pair_in(code, b, start)
+
+        @pl.when(code >= 32)
+        def _():
+            copy = last_in(code, b)
+            copy.start() if start else copy.wait()
 
     def pair_in(code, b, start):
         c, h, array = chip_packed(code), half_in(code), (code // 16) % 2
@@ -473,12 +483,11 @@
 
         lax.fori_loop(0, depth // tile, column, 0)
 
-    def work_x(code, b):
-        index = chip_packed(code) * 2 + half_in(code)
-
+    def x_columns(index, b, here):
         def column(n, _):
             cols = pl.ds(pl.multiple_of(n * tile, tile), tile)
-            new = lax.dot_general(tok[b, :, cols], d[index], BY_ROWS, preferred_element_type=F32)
+            xt = tok[b, here, cols]
+            new = lax.dot_general(xt, d[index, here, :], BY_ROWS, preferred_element_type=F32)
             for i in range(tile // LANES):
                 for j in range(2 * ni):
                     k = (n * (tile // LANES) + i) * ni + j % ni
@@ -487,17 +496,18 @@
 
         lax.fori_loop(0, depth // tile, column, 0)
 
-    def last_x(code):
+    def work_x(code, b):
+        x_columns(chip_packed(code) * 2 + half_in(code), b, slice(None))
+
+    def last_x(code, b):
         c, h = chip_packed(code), half_in(code)
-        own = pltpu.make_async_copy(d.at[c * 2 + h, span(core)], parts.at[4, 0, 0:rows, 0 : 2 * width], tok_sem.at[0, 0])
-        own.start()
+        x_columns(c * 2 + h, b, span(core))
 
         def keep(r):
             there = pl.ds(pl.multiple_of((1 - core) * rows + r.start, 16), 16)
             d_last[r, :] = d[c * 2 + h, there, :]
 
         by_rows(16, rows, keep)
-        own.wait()
         last_to_partner().wait_recv()
 
     def finish_down():
@@ -585,7 +595,7 @@
 
             @pl.when(code >= 32)
             def _():
-                last_x(code)
+                last_x(code, b)
 
             return 0
 
@@ -642,24 +652,9 @@
     term_to_partner(0).wait_send()
 
 
-def finish(
-    dx, wd, acc, d, rows_in, full, parts, to_x, to_gate, to_up, to_down, done, d_in, rows_own, o_sem, d_sem, g_sem
-):
+def finish(dx, wd, acc, d, rows_in, to_x, to_gate, to_up, to_down, done, d_sem, g_sem):
     depth, width = to_gate.shape
-    rows, tile, ni = rows_in.shape[0], 512, width // LANES
-    tp = lax.axis_index("tp")
-    core, y, z = tp % 2, tp // 8, (tp // 2) % 4
-    half, middle = z // 2, ((z + 1) % 4) // 2
-    code = jnp.where(middle == 1, last_code("M"), last_code("C"))
-    ry, rh, mm, h = code % 2, (code // 2) % 2, (code // 4) % 2, code // 8
-    yy, hh = y + ry - 2 * y * ry, half + rh - 2 * half * rh
-    block = (yy * 4 + mm + hh * (3 - 2 * mm)) * 2 + core
-    loads = (
-        pltpu.make_async_copy(full.at[X, block, pl.ds(pl.multiple_of(h * rows, rows), rows)], rows_own, o_sem.at[0]),
-        pltpu.make_async_copy(parts.at[4, 0, 0:rows, 0 : 2 * width], d_in, o_sem.at[1]),
-    )
-    for load in loads:
-        load.start()
+    tile, ni = 512, width // LANES
     copies = []
     for i, (result, place) in enumerate(((dx, to_x), (wd, to_down))):
         n = result.shape[0] // 4
@@ -673,19 +668,15 @@
         here = pl.ds(pl.multiple_of(n * tile, tile), tile)
         return pltpu.make_async_copy(done.at[a, here], (to_gate, to_up)[a].at[here], g_sem.at[a, n])
 
-    for load in loads:
-        load.wait()
-
     def column(n, _):
-        cols = pl.ds(pl.multiple_of(n * tile, tile), tile)
-        new = lax.dot_general(rows_in[:, cols], d[...], BY_ROWS, preferred_element_type=F32)
-        new += lax.dot_general(rows_own[:, cols], d_in[...], BY_ROWS, preferred_element_type=F32)
+        xt = rows_in[:, pl.ds(pl.multiple_of(n * tile, tile), tile)]
+        new = lax.dot_general(xt, d[...], BY_ROWS, preferred_element_type=F32)
         for i in range(tile // LANES):
             to = pl.ds(pl.multiple_of(n * tile + i * LANES, LANES), LANES)
             for j in range(2 * ni):
-                a, k = j // ni, (n * (tile // LANES) + i) * ni + j % ni
-                one = acc[a, k] + new[lanes(i), lanes(j)]
-                done[a, to, j % ni * LANES : (j % ni + 1) * LANES] = one.astype(BF16)
+                k = (n * (tile // LANES) + i) * ni + j % ni
+                one = acc[j // ni, k] + new[lanes(i), lanes(j)]
+                done[j // ni, to, j % ni * LANES : (j % ni + 1) * LANES] = one.astype(BF16)
         for a in range(2):
             store(a, n).start()
         return 0
@@ -714,7 +705,7 @@
                 pltpu.VMEM((rows, 2 * width), BF16),
                 pltpu.VMEM((rows, depth), BF16),
                 jax.ShapeDtypeStruct((2, 2 * chips, block, depth), BF16),
-                jax.ShapeDtypeStruct((5, chips, block, depth), BF16),
+                jax.ShapeDtypeStruct((4, chips, block, depth), BF16),
             ],
             in_specs=[anywhere] * 7,
             out_specs=[inside] * 5 + [anywhere] * 2,
@@ -750,19 +741,16 @@
         return pl.pallas_call(
             finish,
             out_shape=[jax.ShapeDtypeStruct(a.shape, BF16) for a in (dy, w_gate, w_up, w_down)],
-            in_specs=[inside] * 5 + [anywhere] * 2,
+            in_specs=[inside] * 5,
             out_specs=[anywhere] * 4,
             scratch_shapes=[
                 pltpu.VMEM((2, depth, width), BF16),
-                pltpu.VMEM((rows, 2 * width), BF16),
-                pltpu.VMEM((rows, depth), BF16),
-                dma((2,)),
                 dma((2, 4)),
                 dma((2, depth // 512)),
             ],
             compiler_params=pltpu.CompilerParams(vmem_limit_bytes=2**24),
             name="finish",
-        )(*outs)
+        )(*outs[:5])
 
     rows_, cols_ = P(("dp", "tp"), None), P("dp", "tp")
     return jax.shard_map(

time: 411 us -> 410 us (level)
    pallas_call x1, Pallas kernels: 395 us -> 400 us  [step(): pl.pallas_call(kernel, out_shape=[pltpu.VMEM((block, depth), BF16), pltpu...]
    pallas_call x1, Pallas kernels: 9.15 us -> 4.66 us  [step(): pl.pallas_call(finish, out_shape=[jax.ShapeDtypeStruct(a.shape, BF16) for...]
where the time goes in v8:
time: 410 us; the launch traced here: 405 us
  Pallas kernels  404 us (99%)
    pallas_call x1, Pallas kernels, step(): pl.pallas_call(kernel, out_shape=[pltpu.VMEM((block, depth), BF16), pltpu...  400 us

profile of v8, /device:TPU:0, one launch (start us, length us, event | category | flops | bytes accessed | tf_op | source)
XLA Modules:
  0.0 404.8 jit_solution(670347905730177876)
XLA Ops:
  0.6 399.5 %mlp_backward.1 = (bf16[416,2560]{1,0:T(8,128)(2,1)S(1)}, bf16[640,2560]{1,0:T(8,128)(2,1)S(1)}, f32[2,100,128,128]{3,2,1,0:T(8,128)S(1)}, bf16[208,1280]{1,0:T(...) custom-call(bf16[416,2560]{1,0:T(8,128)(2,1)} %x.1, ...), custom_call_target="tpu_custom_call" | custom-call | flops 130862284800 | bytes 204472320 | tf_op jit(solution)/shard_map/mlp_backward/pallas_call | solution.py:699
  400.2 4.7 %finish.1 = (bf16[416,2560]{1,0:T(8,128)(2,1)}, bf16[2560,640]{1,0:T(8,128)(2,1)}, bf16[2560,640]{1,0:T(8,128)(2,1)}, bf16[640,2560]{1,0:T(8,128)(2,1)}) custom-call(bf16[416,2560]{1,0:T(8,128)(2,1)S(1)} %get-tuple-element.9.dx, bf16[640,2560]{1,0:T(8,128)(2,1)S(1)} %get-tuple-element.10.wd, f32[2,100,128,128]{3,2,1,0:T(8,128)S(1)} %get-tuple-element.11.acc, ...), custom_call_target="tpu_custom_call" | custom-call | tf_op jit(solution)/shard_map/finish/pallas_call | solution.py:741

commit v9 on v8

--- a/solution.py
+++ b/solution.py
@@ -18,40 +18,40 @@
 
 START = {
     "a": [
-        "d00C0", "d00M0", "d00M1", "d01C0", "d00C1", "s10M0", "d01M1", "d01C1", "d01M0", "x01M1", "x01C1", "x00M1",
-        "x00C1", "x00M0", "s10M2", "x01C0", "x00C0",
+        "d00C1", "d00M0", "d00C0", "d01C0", "d01M1", "d00M1", "d01C1", "s10M0", "d01M0", "s10M2", "x00M1", "x00C0",
+        "x00C1", "x01C0", "x01M0", "x01M1", "x00M0",
     ],
     "b": [
-        "d00M0", "d00M1", "d01C0", "s10M0", "d01M1", "s10M2", "d01C1", "d01M0", "x01M1", "x01C1", "x00M1", "x11M0",
-        "x00M0", "x01M0", "x01C0", "s00C0", "s00C1",
+        "d00M0", "d00M1", "d01C0", "d01M1", "s10M0", "d01C1", "s10M2", "d01M0", "x01M0", "x00M1", "x00M0", "x01C1",
+        "x01C0", "x11C1", "x01M1", "s00C0", "s00C1",
     ],
     "c": [
-        "d00C0", "x00C0", "d00C1", "x00C1", "s10C0", "s01C0", "s11C0", "s00M0", "s10C1", "s11M1", "s11C1", "s11M0",
-        "s01C1", "s01M0", "x10C7", "s01M1", "s10M3", "s00M1",
+        "d00C0", "x00C0", "d00C1", "s10C1", "x00C1", "s01C0", "s11C0", "s10C0", "s01C1", "s11C1", "s01M1", "s10M3",
+        "s11M1", "s11M0", "x10C7", "s01M0", "s00M0", "s00M1",
     ],
     "d": [
-        "d00M0", "d00C0", "d00M1", "d10M0", "d10M1", "d00C1", "x10M1", "x00M1", "x00C1", "x00M0", "x10M0", "s01C0",
-        "s11C1", "x00C0", "s01C1", "s01M0", "s01M1",
+        "d00M1", "d00C0", "d10M0", "d00C1", "d10M1", "x00M0", "d00M0", "s01C0", "x00C0", "x00C1", "x10M0", "s11C0",
+        "s01C1", "x00M1", "x10M1", "s01M1", "s01M0",
     ],
     "e": [
-        "d00M0", "d00M1", "d01C0", "d00C1", "d00C0", "x00M1", "d01C1", "s10C0", "s11C0", "x00M0", "x01C1", "s11M1",
-        "x00C6", "s11M0", "s10C1", "x01C0", "x00C0", "s10M3",
+        "x00M1", "d00M0", "d00C0", "d00M1", "d00C1", "d01C0", "d01C1", "s10C1", "x00C6", "x00M0", "x01C0", "s11C1",
+        "x01C1", "s10C0", "s11M1", "s11M0", "x00C0", "s10M3",
     ],
 }
 TOKENS = {
     "M": [
-        "0d00M0", "1d00M1", "4d10M0", "4d00C0", "5d01M0", "6d10M1", "6d01C0", "8d11C0", "8d00C1", "9d01M1", "10d11M0", "10d10C1",
-        "12d10C0", "12d11M1", "14d01C1", "16d11C1", "17x00M0", "17x00M1", "18x00C0", "18x00C1", "19x10M1", "19x11M1", "20x01M1", "20x01C1",
-        "22x01M0", "22x10M0", "24x11C1", "24x11M0", "30x01C0", "31x10C1", "33x11C0", "35x10C0",
+        "0d00M0", "1d00M1", "4d00C0", "4d01M1", "6d10M0", "6d01C0", "8d10C0", "8d11M0", "9d00C1", "10d10M1", "10d01C1", "12d10C1",
+        "12d11M1", "14d11C0", "16d11C1", "16d01M0", "17x00M0", "17x00M1", "18x10M1", "18x00C0", "19x00C1", "19x01M0", "20x01C0", "21x10M0",
+        "22x01C1", "23x11C0", "24x11M0", "27x11C1", "30x01M1", "30x10C1", "32x11M1", "35x10C0",
     ],
     "C": [
-        "0d00C0", "1d00C1", "4d10C0", "4d00M0", "6d10M0", "6d00M1", "8d01C0", "8d10M1", "10d11C0", "12d10C1", "12d01M1", "16d11M1",
-        "16d01C1", "18d11C1", "18d01M0", "20d11M0", "21x00C0", "21x00C1", "22x01M1", "22x01C1", "23x11M1", "24x00M1", "24x11C1", "26x10M1",
-        "26x11M0", "28x00M0", "28x10C1", "30x01M0", "30x10M0", "32x01C0", "34x11C0", "36x10C0",
+        "0d00C0", "1d00C1", "4d10C1", "4d00M0", "6d10M0", "6d00M1", "8d01C0", "8d10C0", "10d11C0", "10d01M1", "12d11M1", "14d01C1",
+        "14d10M1", "16d11C1", "18d01M0", "20d11M0", "21x00C0", "21x00C1", "22x01M0", "22x00M1", "24x00M0", "24x10M1", "26x01C1", "26x10C0",
+        "28x01C0", "28x10C1", "30x11C0", "30x11C1", "32x01M1", "32x11M0", "34x11M1", "36x10M0",
     ],
 }
 X_FROM = {"M": 17, "C": 21}
-LAST = {"M": (33, 35), "C": (33, 35)}
+LAST = {"M": (35, 35), "C": (33, 35)}
 STEPS = 37
 
 

time: 410 us -> 410 us (level)
  no operation moved by 1% of the time
where the time goes in v9:
time: 410 us; the launch traced here: 403 us
  Pallas kernels  402 us (98%)
    pallas_call x1, Pallas kernels, step(): pl.pallas_call(kernel, out_shape=[pltpu.VMEM((block, depth), BF16), pltpu...  398 us

profile of v9, /device:TPU:0, one launch (start us, length us, event | category | flops | bytes accessed | tf_op | source)
XLA Modules:
  0.0 403.1 jit_solution(17538416467434264113)
XLA Ops:
  0.6 397.8 %mlp_backward.1 = (bf16[416,2560]{1,0:T(8,128)(2,1)S(1)}, bf16[640,2560]{1,0:T(8,128)(2,1)S(1)}, f32[2,100,128,128]{3,2,1,0:T(8,128)S(1)}, bf16[208,1280]{1,0:T(...) custom-call(bf16[416,2560]{1,0:T(8,128)(2,1)} %x.1, ...), custom_call_target="tpu_custom_call" | custom-call | flops 130862284800 | bytes 204472320 | tf_op jit(solution)/shard_map/mlp_backward/pallas_call | solution.py:699
  398.4 4.7 %finish.1 = (bf16[416,2560]{1,0:T(8,128)(2,1)}, bf16[2560,640]{1,0:T(8,128)(2,1)}, bf16[2560,640]{1,0:T(8,128)(2,1)}, bf16[640,2560]{1,0:T(8,128)(2,1)}) custom-call(bf16[416,2560]{1,0:T(8,128)(2,1)S(1)} %get-tuple-element.9.dx, bf16[640,2560]{1,0:T(8,128)(2,1)S(1)} %get-tuple-element.10.wd, f32[2,100,128,128]{3,2,1,0:T(8,128)S(1)} %get-tuple-element.11.acc, ...), custom_call_target="tpu_custom_call" | custom-call | tf_op jit(solution)/shard_map/finish/pallas_call | solution.py:741
